TPU v7x, 32 devices: a 4x4x1 block of a 4x4x8 slice. The times are simulated.
32 devices in a mesh: dp: 1 (over z), cp: 32 (over y, x, core).
Axes of the slice: x: 4, y: 4, z: 1, core: 2. Of those that a mesh axis runs over, the one named last changes fastest.
The devices are a block of a 4x4x8 slice.
Arguments:
- hidden: bfloat16 [16384, 4096], P(('dp', 'cp'))
- w_q: bfloat16 [4096, 16, 128], replicated
- w_k: bfloat16 [4096, 4, 128], replicated
- w_v: bfloat16 [4096, 4, 128], replicated
- w_o: bfloat16 [16, 128, 4096], replicated
Outputs:
- output: bfloat16 [16384, 4096], P(('dp', 'cp'))
All inputs are finite; a program needn't handle non-finite values.
Results may differ from a plain program's by a relative error of at most 0.00450576.
Values are sent between devices in bfloat16 or wider.
A program may use at most 768 MiB of HBM per device.

v0:
```python
import jax
import jax.numpy as jnp
from jax import lax
from jax.sharding import PartitionSpec as P

WINDOW = 4096
ROPE_BASE = 10000.0


def rotate(values, positions, factor):
    half_dim = values.shape[-1] // 2
    inv_freq = 1.0 / (ROPE_BASE ** (jnp.arange(half_dim, dtype=jnp.float32) * (2.0 / values.shape[-1])))
    angles = positions.astype(jnp.float32)[..., None, None] * inv_freq
    cos_part = jnp.cos(angles)
    sin_part = jnp.sin(angles)
    first_half = values[..., :half_dim].astype(jnp.float32)
    second_half = values[..., half_dim:].astype(jnp.float32)
    rotated = jnp.concatenate([first_half * cos_part - second_half * sin_part, second_half * cos_part + first_half * sin_part], axis=-1)
    return (rotated * factor).astype(jnp.bfloat16)


def band_attention(queries, key_band, val_band, first_pos):
    chunk_len = queries.shape[1]
    band_len = key_band.shape[1] - chunk_len
    q_block = min(chunk_len, 128)
    key_span = band_len + q_block
    row_ids = jnp.arange(q_block)[:, None]
    col_ids = jnp.arange(key_span)[None, :]
    in_band = (col_ids > row_ids) & (col_ids <= row_ids + band_len)

    def one_block(block_id):
        row_start = block_id * q_block
        q_part = lax.dynamic_slice_in_dim(queries, row_start, q_block, axis=1)
        k_part = lax.dynamic_slice_in_dim(key_band, row_start, key_span, axis=1)
        v_part = lax.dynamic_slice_in_dim(val_band, row_start, key_span, axis=1)
        key_pos = first_pos[:, None] + row_start + jnp.arange(key_span)[None, :]
        allowed = in_band[None, :, :] & (key_pos >= 0)[:, None, :]
        scores = jnp.einsum('nqkgd,nskd->nkgqs', q_part, k_part, preferred_element_type=jnp.float32)
        scores = jnp.where(allowed[:, None, None, :, :], scores, -jnp.inf)
        row_max = jnp.max(scores, axis=-1, keepdims=True)
        exp_scores = jnp.exp(scores - row_max)
        row_sum = jnp.sum(exp_scores, axis=-1)
        attn_out = jnp.einsum('nkgqs,nskd->nqkgd', exp_scores.astype(jnp.bfloat16), v_part, preferred_element_type=jnp.float32)
        attn_out = attn_out / jnp.transpose(row_sum, (0, 3, 1, 2))[..., None]
        return attn_out.astype(jnp.bfloat16)

    blocks = lax.map(one_block, jnp.arange(chunk_len // q_block))
    return jnp.moveaxis(blocks, 0, 1).reshape(queries.shape)


def solution(mesh):
    cp_size = mesh.shape['cp']

    def device_step(hidden, w_q, w_k, w_v, w_o):
        my_index = lax.axis_index('cp')
        chunk_len = hidden.shape[0] // 2
        model_dim = hidden.shape[1]
        heads, head_dim = w_q.shape[1], w_q.shape[2]
        kv_heads = w_k.shape[1]
        group_size = heads // kv_heads
        win_chunks = WINDOW // chunk_len
        x_halves = hidden.reshape(2, chunk_len, model_dim)
        chunk_ids = jnp.stack([my_index, 2 * cp_size - 1 - my_index])
        positions = chunk_ids[:, None] * chunk_len + jnp.arange(chunk_len)[None, :]
        key_proj = jnp.einsum('nqd,dhe->nqhe', x_halves, w_k, preferred_element_type=jnp.float32).astype(jnp.bfloat16)
        val_proj = jnp.einsum('nqd,dhe->nqhe', x_halves, w_v, preferred_element_type=jnp.float32).astype(jnp.bfloat16)
        kv_pairs = jnp.stack([rotate(key_proj, positions, 1.0), val_proj], axis=1)
        kv_first = kv_pairs[0]
        kv_second = kv_pairs[1]
        from_below = []
        from_above = []
        from_fold = []
        for offset in range(1, win_chunks + 1):
            from_below.append(lax.ppermute(kv_first, 'cp', [(sender, sender + offset) for sender in range(cp_size - offset)]))
            from_above.append(lax.ppermute(kv_second, 'cp', [(sender, sender - offset) for sender in range(offset, cp_size)]))
            fold_pairs = [(sender, 2 * cp_size - 1 - sender - offset) for sender in range(cp_size - offset, cp_size) if 2 * cp_size - 1 - sender - offset != sender]
            if fold_pairs:
                from_fold.append(lax.ppermute(kv_first, 'cp', fold_pairs))
            else:
                from_fold.append(jnp.zeros_like(kv_first))
        upper_slots = []
        for offset in range(1, win_chunks + 1):
            fold_or_self = jnp.where(2 * cp_size - 1 - my_index - offset == my_index, kv_first, from_fold[offset - 1])
            upper_slots.append(jnp.where(my_index + offset < cp_size, from_above[offset - 1], fold_or_self))
        band_low = jnp.concatenate(from_below[::-1] + [kv_first], axis=1)
        band_high = jnp.concatenate(upper_slots[::-1] + [kv_second], axis=1)
        bands = jnp.stack([band_low, band_high], axis=1)
        q_proj = jnp.einsum('nqd,dhe->nqhe', x_halves, w_q, preferred_element_type=jnp.float32).astype(jnp.bfloat16)
        queries = rotate(q_proj, positions, head_dim ** -0.5).reshape(2, chunk_len, kv_heads, group_size, head_dim)
        first_pos = (chunk_ids - win_chunks) * chunk_len
        attended = band_attention(queries, bands[0], bands[1], first_pos)
        w_out = w_o.reshape(kv_heads, group_size, head_dim, model_dim)
        out_rows = jnp.einsum('nqkge,kgem->nqm', attended, w_out, preferred_element_type=jnp.float32)
        return out_rows.astype(jnp.bfloat16).reshape(2 * chunk_len, model_dim)

    return jax.shard_map(device_step, mesh=mesh, in_specs=(P(('dp', 'cp'), None), P(), P(), P(), P()), out_specs=P(('dp', 'cp'), None), check_vma=False)
```

profile of v0, /device:TPU:125, one launch (start us, length us, event | category | flops | bytes accessed | tf_op | source)
XLA Modules:
  0.0 686.3 jit_solution(9009779341197925625)
XLA Ops:
  0.2 7.4 %copy.17 = bf16[4096,4,128]{0,2,1:T(8,128)(2,1)} copy(bf16[4096,4,128]{2,1,0:T(4,128)(2,1)} %param.9) | data formatting | bytes 8388608 | tf_op args[2]
  24.6 22.0 %copy.21 = bf16[4096,16,128]{0,2,1:T(8,128)(2,1)} copy(bf16[4096,16,128]{2,1,0:T(8,128)(2,1)} %param.8) | data formatting | bytes 33554432 | tf_op args[1]
  46.6 13.7 %fusion.41 = bf16[2,256,16,128]{1,3,2,0:T(8,128)(2,1)S(1)} fusion(bf16[2,256,4096,1]{2,1,3,0:T(8,128)(2,1)} %bitcast.166, bf16[4096,16,128]{0,2,1:T(8,128)(2,1)} %copy.21), kind=kOutput, calls=%fused_computation.49 | convolution fusion | flops 8590983168 | bytes 23068672 | tf_op jit(solution)/shard_map/nqd,dhe->nqhe/dot_general | solution.py:88
  86.9 13.5 %collective-permute-done.5 = bf16[2,256,4,128]{1,3,2,0:T(8,128)(2,1)S(1)} collective-permute-done((bf16[2,256,4,128]{1,3,2,0:T(8,128)(2,1)}, bf16[2,256,4,128]{1,3,2,0:T(8,128)(2,1)S(1)}, u32[]{:S(2)}, u32[]{:S(2)}) %collective-permute-start.5) | collective-permute-done | bytes 524320 | tf_op jit(solution)/shard_map/ppermute | solution.py:74
  103.3 30.8 %collective-permute-start.11 = (bf16[2,256,4,128]{1,3,2,0:T(8,128)(2,1)}, bf16[2,256,4,128]{1,3,2,0:T(8,128)(2,1)S(1)}, u32[]{:S(2)}, u32[]{:S(2)}) collective-permute-start(bf16[2,256,4,128]{1,3,2,0:T(8,128)(2,1)} %get-tuple-element.108), channel_id=1, source_target_pairs={{0,5},{1,6},{2,7},{3,8},{4,9},{5,10},{6,11},{7,12},{8,13},{9,14},{... | collective-permute-start | bytes 1572872 | tf_op jit(solution)/shard_map/ppermute | solution.py:74
  134.1 6.2 collective-permute-done.7
  140.3 17.7 %collective-permute-start.12 = (bf16[2,256,4,128]{1,3,2,0:T(8,128)(2,1)}, bf16[2,256,4,128]{1,3,2,0:T(8,128)(2,1)S(1)}, u32[]{:S(2)}, u32[]{:S(2)}) collective-permute-start(bf16[2,256,4,128]{1,3,2,0:T(8,128)(2,1)} %get-tuple-element.108), channel_id=1, source_target_pairs={{0,4},{1,5},{2,6},{3,7},{4,8},{5,9},{6,10},{7,11},{8,12},{9,13},{1... | collective-permute-start | bytes 1572872 | tf_op jit(solution)/shard_map/ppermute | solution.py:74
  158.1 22.7 %collective-permute-start.13 = (bf16[2,256,4,128]{1,3,2,0:T(8,128)(2,1)}, bf16[2,256,4,128]{1,3,2,0:T(8,128)(2,1)S(1)}, u32[]{:S(2)}, u32[]{:S(2)}) collective-permute-start(bf16[2,256,4,128]{1,3,2,0:T(8,128)(2,1)} %get-tuple-element.108), channel_id=1, source_target_pairs={{0,3},{1,4},{2,5},{3,6},{4,7},{5,8},{6,9},{7,10},{8,11},{9,12},{10... | collective-permute-start | bytes 1572872 | tf_op jit(solution)/shard_map/ppermute | solution.py:74
  180.8 8.0 %collective-permute-start.14 = (bf16[2,256,4,128]{1,3,2,0:T(8,128)(2,1)}, bf16[2,256,4,128]{1,3,2,0:T(8,128)(2,1)S(1)}, u32[]{:S(2)}, u32[]{:S(2)}) collective-permute-start(bf16[2,256,4,128]{1,3,2,0:T(8,128)(2,1)} %get-tuple-element.108), channel_id=1, source_target_pairs={{0,2},{1,3},{2,4},{3,5},{4,6},{5,7},{6,8},{7,9},{8,10},{9,11},{10,... | collective-permute-start | bytes 1572872 | tf_op jit(solution)/shard_map/ppermute | solution.py:74
  188.9 7.3 %collective-permute-start.15 = (bf16[2,256,4,128]{1,3,2,0:T(8,128)(2,1)}, bf16[2,256,4,128]{1,3,2,0:T(8,128)(2,1)S(1)}, u32[]{:S(2)}, u32[]{:S(2)}) collective-permute-start(bf16[2,256,4,128]{1,3,2,0:T(8,128)(2,1)} %get-tuple-element.108), channel_id=1, source_target_pairs={{0,1},{1,2},{2,3},{3,4},{4,5},{5,6},{6,7},{7,8},{8,9},{9,10},{10,1... | collective-permute-start | bytes 1572872 | tf_op jit(solution)/shard_map/ppermute | solution.py:74
  207.1 6.9 %collective-permute-start.20 = (bf16[2,256,4,128]{1,3,2,0:T(8,128)(2,1)S(1)}, bf16[2,256,4,128]{1,3,2,0:T(8,128)(2,1)S(1)}, u32[]{:S(2)}, u32[]{:S(2)}) collective-permute-start(bf16[2,256,4,128]{1,3,2,0:T(8,128)(2,1)S(1)} %copy-done), channel_id=1, source_target_pairs={{14,0},{15,1},{16,2},{17,3},{18,4},{19,5},{20,6},{21,7},{22,8},{23... | collective-permute-start | bytes 1572872 | tf_op jit(solution)/shard_map/ppermute | solution.py:75
  214.1 31.6 %collective-permute-done.16 = bf16[2,256,4,128]{1,3,2,0:T(8,128)(2,1)S(1)} collective-permute-done((bf16[2,256,4,128]{1,3,2,0:T(8,128)(2,1)S(1)}, bf16[2,256,4,128]{1,3,2,0:T(8,128)(2,1)S(1)}, u32[]{:S(2)}, u32[]{:S(2)}) %collective-permute-start.16) | collective-permute-done | bytes 524320 | tf_op jit(solution)/shard_map/ppermute | solution.py:75
  259.6 63.1 %collective-permute-start.25 = (bf16[2,256,4,128]{1,3,2,0:T(8,128)(2,1)}, bf16[2,256,4,128]{1,3,2,0:T(8,128)(2,1)S(1)}, u32[]{:S(2)}, u32[]{:S(2)}) collective-permute-start(bf16[2,256,4,128]{1,3,2,0:T(8,128)(2,1)} %get-tuple-element.108), channel_id=1, source_target_pairs={{20,31},{21,30},{22,29},{23,28},{24,27},{25,26},{26,25},{27,24},{2... | collective-permute-start | bytes 1572872 | tf_op jit(solution)/shard_map/ppermute | solution.py:78
  335.3 13.3 %collective-permute-done.25 = bf16[2,256,4,128]{1,3,2,0:T(8,128)(2,1)S(1)} collective-permute-done((bf16[2,256,4,128]{1,3,2,0:T(8,128)(2,1)}, bf16[2,256,4,128]{1,3,2,0:T(8,128)(2,1)S(1)}, u32[]{:S(2)}, u32[]{:S(2)}) %collective-permute-start.25) | collective-permute-done | bytes 524320 | tf_op jit(solution)/shard_map/ppermute | solution.py:78
  361.3 13.9 %collective-permute-start.33 = (bf16[2,256,4,128]{1,3,2,0:T(8,128)(2,1)}, bf16[2,256,4,128]{1,3,2,0:T(8,128)(2,1)S(1)}, u32[]{:S(2)}, u32[]{:S(2)}) collective-permute-start(bf16[2,256,4,128]{1,3,2,0:T(8,128)(2,1)} %get-tuple-element.108), channel_id=1, source_target_pairs={{24,31},{25,30},{26,29},{27,28},{28,27},{29,26},{30,25},{31,24}} | collective-permute-start | bytes 1572872 | tf_op jit(solution)/shard_map/ppermute | solution.py:78
  382.8 21.1 %collective-permute-start.36 = (bf16[2,256,4,128]{1,3,2,0:T(8,128)(2,1)S(1)}, bf16[2,256,4,128]{1,3,2,0:T(8,128)(2,1)S(1)}, u32[]{:S(2)}, u32[]{:S(2)}) collective-permute-start(bf16[2,256,4,128]{1,3,2,0:T(8,128)(2,1)S(1)} %copy-done), channel_id=1, source_target_pairs={{6,0},{7,1},{8,2},{9,3},{10,4},{11,5},{12,6},{13,7},{14,8},{15,9},... | collective-permute-start | bytes 1572872 | tf_op jit(solution)/shard_map/ppermute | solution.py:75
  406.4 20.0 %collective-permute-start.38 = (bf16[2,256,4,128]{1,3,2,0:T(8,128)(2,1)S(1)}, bf16[2,256,4,128]{1,3,2,0:T(8,128)(2,1)S(1)}, u32[]{:S(2)}, u32[]{:S(2)}) collective-permute-start(bf16[2,256,4,128]{1,3,2,0:T(8,128)(2,1)S(1)} %copy-done), channel_id=1, source_target_pairs={{5,0},{6,1},{7,2},{8,3},{9,4},{10,5},{11,6},{12,7},{13,8},{14,9},{... | collective-permute-start | bytes 1572872 | tf_op jit(solution)/shard_map/ppermute | solution.py:75
  427.4 9.7 %collective-permute-start.40 = (bf16[2,256,4,128]{1,3,2,0:T(8,128)(2,1)S(1)}, bf16[2,256,4,128]{1,3,2,0:T(8,128)(2,1)S(1)}, u32[]{:S(2)}, u32[]{:S(2)}) collective-permute-start(bf16[2,256,4,128]{1,3,2,0:T(8,128)(2,1)S(1)} %copy-done), channel_id=1, source_target_pairs={{4,0},{5,1},{6,2},{7,3},{8,4},{9,5},{10,6},{11,7},{12,8},{13,9},{1... | collective-permute-start | bytes 1572872 | tf_op jit(solution)/shard_map/ppermute | solution.py:75
  440.5 7.0 %collective-permute-start.42 = (bf16[2,256,4,128]{1,3,2,0:T(8,128)(2,1)S(1)}, bf16[2,256,4,128]{1,3,2,0:T(8,128)(2,1)S(1)}, u32[]{:S(2)}, u32[]{:S(2)}) collective-permute-start(bf16[2,256,4,128]{1,3,2,0:T(8,128)(2,1)S(1)} %copy-done), channel_id=1, source_target_pairs={{3,0},{4,1},{5,2},{6,3},{7,4},{8,5},{9,6},{10,7},{11,8},{12,9},{13... | collective-permute-start | bytes 1572872 | tf_op jit(solution)/shard_map/ppermute | solution.py:75
  450.7 10.1 %collective-permute-start.44 = (bf16[2,256,4,128]{1,3,2,0:T(8,128)(2,1)S(1)}, bf16[2,256,4,128]{1,3,2,0:T(8,128)(2,1)S(1)}, u32[]{:S(2)}, u32[]{:S(2)}) collective-permute-start(bf16[2,256,4,128]{1,3,2,0:T(8,128)(2,1)S(1)} %copy-done), channel_id=1, source_target_pairs={{2,0},{3,1},{4,2},{5,3},{6,4},{7,5},{8,6},{9,7},{10,8},{11,9},{12,... | collective-permute-start | bytes 1572872 | tf_op jit(solution)/shard_map/ppermute | solution.py:75
  465.8 13.6 %collective-permute-start.46 = (bf16[2,256,4,128]{1,3,2,0:T(8,128)(2,1)S(1)}, bf16[2,256,4,128]{1,3,2,0:T(8,128)(2,1)S(1)}, u32[]{:S(2)}, u32[]{:S(2)}) collective-permute-start(bf16[2,256,4,128]{1,3,2,0:T(8,128)(2,1)S(1)} %copy-done), channel_id=1, source_target_pairs={{1,0},{2,1},{3,2},{4,3},{5,4},{6,5},{7,6},{8,7},{9,8},{10,9},{11,1... | collective-permute-start | bytes 1572872 | tf_op jit(solution)/shard_map/ppermute | solution.py:75
  479.7 12.3 %collective-permute-done.43 = bf16[2,256,4,128]{1,3,2,0:T(8,128)(2,1)S(1)} collective-permute-done((bf16[2,256,4,128]{1,3,2,0:T(8,128)(2,1)}, bf16[2,256,4,128]{1,3,2,0:T(8,128)(2,1)S(1)}, u32[]{:S(2)}, u32[]{:S(2)}) %collective-permute-start.43) | collective-permute-done | bytes 524320 | tf_op jit(solution)/shard_map/ppermute | solution.py:78
  492.3 9.0 %collective-permute-done.44 = bf16[2,256,4,128]{1,3,2,0:T(8,128)(2,1)S(1)} collective-permute-done((bf16[2,256,4,128]{1,3,2,0:T(8,128)(2,1)S(1)}, bf16[2,256,4,128]{1,3,2,0:T(8,128)(2,1)S(1)}, u32[]{:S(2)}, u32[]{:S(2)}) %collective-permute-start.44) | collective-permute-done | bytes 524320 | tf_op jit(solution)/shard_map/ppermute | solution.py:75
  501.8 6.5 fusion.32
  508.3 164.5 %while.11 = (s32[]{:T(128)}, bf16[2,2,128,4,4,128]{5,2,0,4,1,3:T(8,128)(2,1)}, s32[2]{0:T(128)S(1)}, bf16[2,4352,4,128]{1,3,2,0:T(8,128)(2,1)}, s32[2]{0:T(128)S...) while((s32[]{:T(128)}, ...), condition=%wide.region_3.4_spmd.clone, body=%wide.region_0.3_spmd.clone.sunk | while | flops 9000542208 | bytes 236717808 | solution.py:47
  511.6 28.0 %fusion.73 = (f32[2,4,4,128]{3,2,1,0:T(4,128)S(1)}, f32[2,4,4224,128,4]{3,2,4,1,0:T(8,128)}) fusion(pred[2,128,4224]{1,2,0:T(8,128)(4,1)S(1)} %broadcast_and_fusion.2, bf16[2,256,4,4,128]{4,1,3,2,0:T(8,128)(2,1)} %get-tuple-element.200, s32[]{:T(128)S(6)} %select_n.358, bf16[2,4352,4,128]{1,3,2,0:T(8,128)(2,1)} %get-tuple-element.199, s32[]{:T(128)S(6)} %select_n.359), kind=kOutput, calls=%fused_computation.3.clone.1 | convolution fusion | flops 4463783936 | bytes 80003080 | tf_op jit(solution)/shard_map/while/body/eval_jaxpr/nqkgd,nskd->nkgqs/dot_general | solution.py:38
  539.6 21.8 %fusion.74 = f32[2,4,4,128]{3,2,1,0:T(4,128)S(1)} fusion(f32[2,4,4224,128,4]{3,2,4,1,0:T(8,128)} %get-tuple-element.166, f32[2,4,4,128]{3,2,1,0:T(4,128)S(1)} %get-tuple-element.167, pred[2,128,4224]{1,2,0:T(8,128)(4,1)S(1)} %broadcast_and_fusion.2), kind=kLoop, calls=%fused_computation.4.clone.1 | loop fusion | flops 51900416 | bytes 70320128 | tf_op jit(solution)/shard_map/while/body/eval_jaxpr/reduce_sum | solution.py:42
  561.4 27.2 %fusion.75 = bf16[1,2,128,4,4,128]{2,5,4,3,1,0:T(8,128)(2,1)S(1)} fusion(f32[2,4,4224,128,4]{3,2,4,1,0:T(8,128)} %get-tuple-element.166, f32[2,4,4,128]{3,2,1,0:T(4,128)S(1)} %get-tuple-element.167, pred[2,128,4224]{1,2,0:T(8,128)(4,1)S(1)} %broadcast_and_fusion.2, bf16[2,4352,4,128]{1,3,2,0:T(8,128)(2,1)} %get-tuple-element.197, ...), kind=kOutput, calls=%fused_computation.19.clone.1 | convolution fusion | flops 4482138112 | bytes 80019456 | tf_op jit(solution)/shard_map/while/body/eval_jaxpr/nkgqs,nskd->nqkgd/dot_general | solution.py:43
  593.9 28.0 %fusion.73 = (f32[2,4,4,128]{3,2,1,0:T(4,128)S(1)}, f32[2,4,4224,128,4]{3,2,4,1,0:T(8,128)}) fusion(pred[2,128,4224]{1,2,0:T(8,128)(4,1)S(1)} %broadcast_and_fusion.2, bf16[2,256,4,4,128]{4,1,3,2,0:T(8,128)(2,1)} %get-tuple-element.200, s32[]{:T(128)S(6)} %select_n.358, bf16[2,4352,4,128]{1,3,2,0:T(8,128)(2,1)} %get-tuple-element.199, s32[]{:T(128)S(6)} %select_n.359), kind=kOutput, calls=%fused_computation.3.clone.1 | convolution fusion | flops 4463783936 | bytes 80003080 | tf_op jit(solution)/shard_map/while/body/eval_jaxpr/nqkgd,nskd->nkgqs/dot_general | solution.py:38
  621.9 21.8 %fusion.74 = f32[2,4,4,128]{3,2,1,0:T(4,128)S(1)} fusion(f32[2,4,4224,128,4]{3,2,4,1,0:T(8,128)} %get-tuple-element.166, f32[2,4,4,128]{3,2,1,0:T(4,128)S(1)} %get-tuple-element.167, pred[2,128,4224]{1,2,0:T(8,128)(4,1)S(1)} %broadcast_and_fusion.2), kind=kLoop, calls=%fused_computation.4.clone.1 | loop fusion | flops 51900416 | bytes 70320128 | tf_op jit(solution)/shard_map/while/body/eval_jaxpr/reduce_sum | solution.py:42
  643.6 27.2 %fusion.75 = bf16[1,2,128,4,4,128]{2,5,4,3,1,0:T(8,128)(2,1)S(1)} fusion(f32[2,4,4224,128,4]{3,2,4,1,0:T(8,128)} %get-tuple-element.166, f32[2,4,4,128]{3,2,1,0:T(4,128)S(1)} %get-tuple-element.167, pred[2,128,4224]{1,2,0:T(8,128)(4,1)S(1)} %broadcast_and_fusion.2, bf16[2,4352,4,128]{1,3,2,0:T(8,128)(2,1)} %get-tuple-element.197, ...), kind=kOutput, calls=%fused_computation.19.clone.1 | convolution fusion | flops 4482138112 | bytes 80019456 | tf_op jit(solution)/shard_map/while/body/eval_jaxpr/nkgqs,nskd->nqkgd/dot_general | solution.py:43
  672.8 13.5 %bitcast_convert_fusion = bf16[2,256,4096]{2,1,0:T(8,128)(2,1)} fusion(bf16[2,256,4,4,128]{4,1,3,0,2:T(8,128)(2,1)} %bitcast.168, bf16[4,4,128,4096,1]{3,2,1,4,0:T(8,128)(2,1)} %bitcast.164), kind=kOutput, calls=%fused_computation.35 | convolution fusion | flops 8592031744 | bytes 23068672 | tf_op jit(solution)/shard_map/nqkge,kgem->nqm/dot_general | solution.py:93
  (143 shorter events, 129.4 us)
Async XLA Ops:
  17.8 57.0 %collective-permute-start = (bf16[2,256,4,128]{1,3,2,0:T(8,128)(2,1)}, bf16[2,256,4,128]{1,3,2,0:T(8,128)(2,1)}, u32[]{:S(2)}, u32[]{:S(2)}) collective-permute-start(bf16[2,256,4,128]{1,3,2,0:T(8,128)(2,1)} %get-tuple-element.108), channel_id=1, source_target_pairs={{0,16},{1,17},{2,18},{3,19},{4,20},{5,21},{6,22},{7,23},{8,24},{9,... | collective-permute-start | bytes 1572872 | tf_op jit(solution)/shard_map/ppermute | solution.py:74
  19.1 58.1 %collective-permute-start.1 = (bf16[2,256,4,128]{1,3,2,0:T(8,128)(2,1)}, bf16[2,256,4,128]{1,3,2,0:T(8,128)(2,1)}, u32[]{:S(2)}, u32[]{:S(2)}) collective-permute-start(bf16[2,256,4,128]{1,3,2,0:T(8,128)(2,1)} %get-tuple-element.108), channel_id=1, source_target_pairs={{0,15},{1,16},{2,17},{3,18},{4,19},{5,20},{6,21},{7,22},{8,23},{9,... | collective-permute-start | bytes 1572872 | tf_op jit(solution)/shard_map/ppermute | solution.py:74
  20.5 58.1 %collective-permute-start.2 = (bf16[2,256,4,128]{1,3,2,0:T(8,128)(2,1)}, bf16[2,256,4,128]{1,3,2,0:T(8,128)(2,1)}, u32[]{:S(2)}, u32[]{:S(2)}) collective-permute-start(bf16[2,256,4,128]{1,3,2,0:T(8,128)(2,1)} %get-tuple-element.108), channel_id=1, source_target_pairs={{0,14},{1,15},{2,16},{3,17},{4,18},{5,19},{6,20},{7,21},{8,22},{9,... | collective-permute-start | bytes 1572872 | tf_op jit(solution)/shard_map/ppermute | solution.py:74
  21.8 60.3 %collective-permute-start.3 = (bf16[2,256,4,128]{1,3,2,0:T(8,128)(2,1)}, bf16[2,256,4,128]{1,3,2,0:T(8,128)(2,1)}, u32[]{:S(2)}, u32[]{:S(2)}) collective-permute-start(bf16[2,256,4,128]{1,3,2,0:T(8,128)(2,1)} %get-tuple-element.108), channel_id=1, source_target_pairs={{0,13},{1,14},{2,15},{3,16},{4,17},{5,18},{6,19},{7,20},{8,21},{9,... | collective-permute-start | bytes 1572872 | tf_op jit(solution)/shard_map/ppermute | solution.py:74
  23.1 61.4 %collective-permute-start.4 = (bf16[2,256,4,128]{1,3,2,0:T(8,128)(2,1)}, bf16[2,256,4,128]{1,3,2,0:T(8,128)(2,1)}, u32[]{:S(2)}, u32[]{:S(2)}) collective-permute-start(bf16[2,256,4,128]{1,3,2,0:T(8,128)(2,1)} %get-tuple-element.108), channel_id=1, source_target_pairs={{0,12},{1,13},{2,14},{3,15},{4,16},{5,17},{6,18},{7,19},{8,20},{9,... | collective-permute-start | bytes 1572872 | tf_op jit(solution)/shard_map/ppermute | solution.py:74
  78.6 61.7 %collective-permute-start.7 = (bf16[2,256,4,128]{1,3,2,0:T(8,128)(2,1)}, bf16[2,256,4,128]{1,3,2,0:T(8,128)(2,1)S(1)}, u32[]{:S(2)}, u32[]{:S(2)}) collective-permute-start(bf16[2,256,4,128]{1,3,2,0:T(8,128)(2,1)} %get-tuple-element.108), channel_id=1, source_target_pairs={{0,9},{1,10},{2,11},{3,12},{4,13},{5,14},{6,15},{7,16},{8,17},{9,1... | collective-permute-start | bytes 1572872 | tf_op jit(solution)/shard_map/ppermute | solution.py:74
  82.1 76.0 %collective-permute-start.8 = (bf16[2,256,4,128]{1,3,2,0:T(8,128)(2,1)}, bf16[2,256,4,128]{1,3,2,0:T(8,128)(2,1)S(1)}, u32[]{:S(2)}, u32[]{:S(2)}) collective-permute-start(bf16[2,256,4,128]{1,3,2,0:T(8,128)(2,1)} %get-tuple-element.108), channel_id=1, source_target_pairs={{0,8},{1,9},{2,10},{3,11},{4,12},{5,13},{6,14},{7,15},{8,16},{9,17... | collective-permute-start | bytes 1572872 | tf_op jit(solution)/shard_map/ppermute | solution.py:74
  84.5 96.3 %collective-permute-start.9 = (bf16[2,256,4,128]{1,3,2,0:T(8,128)(2,1)}, bf16[2,256,4,128]{1,3,2,0:T(8,128)(2,1)S(1)}, u32[]{:S(2)}, u32[]{:S(2)}) collective-permute-start(bf16[2,256,4,128]{1,3,2,0:T(8,128)(2,1)} %get-tuple-element.108), channel_id=1, source_target_pairs={{0,7},{1,8},{2,9},{3,10},{4,11},{5,12},{6,13},{7,14},{8,15},{9,16}... | collective-permute-start | bytes 1572872 | tf_op jit(solution)/shard_map/ppermute | solution.py:74
  100.3 88.5 %collective-permute-start.10 = (bf16[2,256,4,128]{1,3,2,0:T(8,128)(2,1)}, bf16[2,256,4,128]{1,3,2,0:T(8,128)(2,1)S(1)}, u32[]{:S(2)}, u32[]{:S(2)}) collective-permute-start(bf16[2,256,4,128]{1,3,2,0:T(8,128)(2,1)} %get-tuple-element.108), channel_id=1, source_target_pairs={{0,6},{1,7},{2,8},{3,9},{4,10},{5,11},{6,12},{7,13},{8,14},{9,15},... | collective-permute-start | bytes 1572872 | tf_op jit(solution)/shard_map/ppermute | solution.py:74
  103.3 93.0 %collective-permute-start.11 = (bf16[2,256,4,128]{1,3,2,0:T(8,128)(2,1)}, bf16[2,256,4,128]{1,3,2,0:T(8,128)(2,1)S(1)}, u32[]{:S(2)}, u32[]{:S(2)}) collective-permute-start(bf16[2,256,4,128]{1,3,2,0:T(8,128)(2,1)} %get-tuple-element.108), channel_id=1, source_target_pairs={{0,5},{1,6},{2,7},{3,8},{4,9},{5,10},{6,11},{7,12},{8,13},{9,14},{... | collective-permute-start | bytes 1572872 | tf_op jit(solution)/shard_map/ppermute | solution.py:74
  140.3 58.5 %collective-permute-start.12 = (bf16[2,256,4,128]{1,3,2,0:T(8,128)(2,1)}, bf16[2,256,4,128]{1,3,2,0:T(8,128)(2,1)S(1)}, u32[]{:S(2)}, u32[]{:S(2)}) collective-permute-start(bf16[2,256,4,128]{1,3,2,0:T(8,128)(2,1)} %get-tuple-element.108), channel_id=1, source_target_pairs={{0,4},{1,5},{2,6},{3,7},{4,8},{5,9},{6,10},{7,11},{8,12},{9,13},{1... | collective-permute-start | bytes 1572872 | tf_op jit(solution)/shard_map/ppermute | solution.py:74
  158.1 42.2 %collective-permute-start.13 = (bf16[2,256,4,128]{1,3,2,0:T(8,128)(2,1)}, bf16[2,256,4,128]{1,3,2,0:T(8,128)(2,1)S(1)}, u32[]{:S(2)}, u32[]{:S(2)}) collective-permute-start(bf16[2,256,4,128]{1,3,2,0:T(8,128)(2,1)} %get-tuple-element.108), channel_id=1, source_target_pairs={{0,3},{1,4},{2,5},{3,6},{4,7},{5,8},{6,9},{7,10},{8,11},{9,12},{10... | collective-permute-start | bytes 1572872 | tf_op jit(solution)/shard_map/ppermute | solution.py:74
  196.2 53.4 %collective-permute-start.17 = (bf16[2,256,4,128]{1,3,2,0:T(8,128)(2,1)}, bf16[2,256,4,128]{1,3,2,0:T(8,128)(2,1)S(1)}, u32[]{:S(2)}, u32[]{:S(2)}) collective-permute-start(bf16[2,256,4,128]{1,3,2,0:T(8,128)(2,1)} %get-tuple-element.108), channel_id=1, source_target_pairs={{16,31},{17,30},{18,29},{19,28},{20,27},{21,26},{22,25},{23,24},{2... | collective-permute-start | bytes 1572872 | tf_op jit(solution)/shard_map/ppermute | solution.py:78
  198.8 46.9 %collective-permute-start.16 = (bf16[2,256,4,128]{1,3,2,0:T(8,128)(2,1)S(1)}, bf16[2,256,4,128]{1,3,2,0:T(8,128)(2,1)S(1)}, u32[]{:S(2)}, u32[]{:S(2)}) collective-permute-start(bf16[2,256,4,128]{1,3,2,0:T(8,128)(2,1)S(1)} %copy-done), channel_id=1, source_target_pairs={{16,0},{17,1},{18,2},{19,3},{20,4},{21,5},{22,6},{23,7},{24,8},{25... | collective-permute-start | bytes 1572872 | tf_op jit(solution)/shard_map/ppermute | solution.py:75
  200.3 50.9 %collective-permute-start.18 = (bf16[2,256,4,128]{1,3,2,0:T(8,128)(2,1)S(1)}, bf16[2,256,4,128]{1,3,2,0:T(8,128)(2,1)S(1)}, u32[]{:S(2)}, u32[]{:S(2)}) collective-permute-start(bf16[2,256,4,128]{1,3,2,0:T(8,128)(2,1)S(1)} %copy-done), channel_id=1, source_target_pairs={{15,0},{16,1},{17,2},{18,3},{19,4},{20,5},{21,6},{22,7},{23,8},{24... | collective-permute-start | bytes 1572872 | tf_op jit(solution)/shard_map/ppermute | solution.py:75
  203.1 54.2 %collective-permute-start.19 = (bf16[2,256,4,128]{1,3,2,0:T(8,128)(2,1)}, bf16[2,256,4,128]{1,3,2,0:T(8,128)(2,1)S(1)}, u32[]{:S(2)}, u32[]{:S(2)}) collective-permute-start(bf16[2,256,4,128]{1,3,2,0:T(8,128)(2,1)} %get-tuple-element.108), channel_id=1, source_target_pairs={{17,31},{18,30},{19,29},{20,28},{21,27},{22,26},{23,25},{25,23},{2... | collective-permute-start | bytes 1572872 | tf_op jit(solution)/shard_map/ppermute | solution.py:78
  207.1 52.5 %collective-permute-start.20 = (bf16[2,256,4,128]{1,3,2,0:T(8,128)(2,1)S(1)}, bf16[2,256,4,128]{1,3,2,0:T(8,128)(2,1)S(1)}, u32[]{:S(2)}, u32[]{:S(2)}) collective-permute-start(bf16[2,256,4,128]{1,3,2,0:T(8,128)(2,1)S(1)} %copy-done), channel_id=1, source_target_pairs={{14,0},{15,1},{16,2},{17,3},{18,4},{19,5},{20,6},{21,7},{22,8},{23... | collective-permute-start | bytes 1572872 | tf_op jit(solution)/shard_map/ppermute | solution.py:75
  245.7 77.1 %collective-permute-start.21 = (bf16[2,256,4,128]{1,3,2,0:T(8,128)(2,1)}, bf16[2,256,4,128]{1,3,2,0:T(8,128)(2,1)S(1)}, u32[]{:S(2)}, u32[]{:S(2)}) collective-permute-start(bf16[2,256,4,128]{1,3,2,0:T(8,128)(2,1)} %get-tuple-element.108), channel_id=1, source_target_pairs={{18,31},{19,30},{20,29},{21,28},{22,27},{23,26},{24,25},{25,24},{2... | collective-permute-start | bytes 1572872 | tf_op jit(solution)/shard_map/ppermute | solution.py:78
  249.6 74.8 %collective-permute-start.22 = (bf16[2,256,4,128]{1,3,2,0:T(8,128)(2,1)S(1)}, bf16[2,256,4,128]{1,3,2,0:T(8,128)(2,1)S(1)}, u32[]{:S(2)}, u32[]{:S(2)}) collective-permute-start(bf16[2,256,4,128]{1,3,2,0:T(8,128)(2,1)S(1)} %copy-done), channel_id=1, source_target_pairs={{13,0},{14,1},{15,2},{16,3},{17,4},{18,5},{19,6},{20,7},{21,8},{22... | collective-permute-start | bytes 1572872 | tf_op jit(solution)/shard_map/ppermute | solution.py:75
  251.2 77.8 %collective-permute-start.23 = (bf16[2,256,4,128]{1,3,2,0:T(8,128)(2,1)}, bf16[2,256,4,128]{1,3,2,0:T(8,128)(2,1)S(1)}, u32[]{:S(2)}, u32[]{:S(2)}) collective-permute-start(bf16[2,256,4,128]{1,3,2,0:T(8,128)(2,1)} %get-tuple-element.108), channel_id=1, source_target_pairs={{19,31},{20,30},{21,29},{22,28},{23,27},{24,26},{26,24},{27,23},{2... | collective-permute-start | bytes 1572872 | tf_op jit(solution)/shard_map/ppermute | solution.py:78
  257.3 73.2 %collective-permute-start.24 = (bf16[2,256,4,128]{1,3,2,0:T(8,128)(2,1)S(1)}, bf16[2,256,4,128]{1,3,2,0:T(8,128)(2,1)S(1)}, u32[]{:S(2)}, u32[]{:S(2)}) collective-permute-start(bf16[2,256,4,128]{1,3,2,0:T(8,128)(2,1)S(1)} %copy-done), channel_id=1, source_target_pairs={{12,0},{13,1},{14,2},{15,3},{16,4},{17,5},{18,6},{19,7},{20,8},{21... | collective-permute-start | bytes 1572872 | tf_op jit(solution)/shard_map/ppermute | solution.py:75
  259.6 88.9 %collective-permute-start.25 = (bf16[2,256,4,128]{1,3,2,0:T(8,128)(2,1)}, bf16[2,256,4,128]{1,3,2,0:T(8,128)(2,1)S(1)}, u32[]{:S(2)}, u32[]{:S(2)}) collective-permute-start(bf16[2,256,4,128]{1,3,2,0:T(8,128)(2,1)} %get-tuple-element.108), channel_id=1, source_target_pairs={{20,31},{21,30},{22,29},{23,28},{24,27},{25,26},{26,25},{27,24},{2... | collective-permute-start | bytes 1572872 | tf_op jit(solution)/shard_map/ppermute | solution.py:78
  330.6 44.6 %collective-permute-start.29 = (bf16[2,256,4,128]{1,3,2,0:T(8,128)(2,1)}, bf16[2,256,4,128]{1,3,2,0:T(8,128)(2,1)S(1)}, u32[]{:S(2)}, u32[]{:S(2)}) collective-permute-start(bf16[2,256,4,128]{1,3,2,0:T(8,128)(2,1)} %get-tuple-element.108), channel_id=1, source_target_pairs={{22,31},{23,30},{24,29},{25,28},{26,27},{27,26},{28,25},{29,24},{3... | collective-permute-start | bytes 1572872 | tf_op jit(solution)/shard_map/ppermute | solution.py:78
  359.7 44.3 %collective-permute-start.32 = (bf16[2,256,4,128]{1,3,2,0:T(8,128)(2,1)S(1)}, bf16[2,256,4,128]{1,3,2,0:T(8,128)(2,1)S(1)}, u32[]{:S(2)}, u32[]{:S(2)}) collective-permute-start(bf16[2,256,4,128]{1,3,2,0:T(8,128)(2,1)S(1)} %copy-done), channel_id=1, source_target_pairs={{8,0},{9,1},{10,2},{11,3},{12,4},{13,5},{14,6},{15,7},{16,8},{17,9... | collective-permute-start | bytes 1572872 | tf_op jit(solution)/shard_map/ppermute | solution.py:75
  361.3 45.1 %collective-permute-start.33 = (bf16[2,256,4,128]{1,3,2,0:T(8,128)(2,1)}, bf16[2,256,4,128]{1,3,2,0:T(8,128)(2,1)S(1)}, u32[]{:S(2)}, u32[]{:S(2)}) collective-permute-start(bf16[2,256,4,128]{1,3,2,0:T(8,128)(2,1)} %get-tuple-element.108), channel_id=1, source_target_pairs={{24,31},{25,30},{26,29},{27,28},{28,27},{29,26},{30,25},{31,24}} | collective-permute-start | bytes 1572872 | tf_op jit(solution)/shard_map/ppermute | solution.py:78
  375.2 51.4 %collective-permute-start.34 = (bf16[2,256,4,128]{1,3,2,0:T(8,128)(2,1)S(1)}, bf16[2,256,4,128]{1,3,2,0:T(8,128)(2,1)S(1)}, u32[]{:S(2)}, u32[]{:S(2)}) collective-permute-start(bf16[2,256,4,128]{1,3,2,0:T(8,128)(2,1)S(1)} %copy-done), channel_id=1, source_target_pairs={{7,0},{8,1},{9,2},{10,3},{11,4},{12,5},{13,6},{14,7},{15,8},{16,9}... | collective-permute-start | bytes 1572872 | tf_op jit(solution)/shard_map/ppermute | solution.py:75
  378.2 49.2 %collective-permute-start.35 = (bf16[2,256,4,128]{1,3,2,0:T(8,128)(2,1)}, bf16[2,256,4,128]{1,3,2,0:T(8,128)(2,1)S(1)}, u32[]{:S(2)}, u32[]{:S(2)}) collective-permute-start(bf16[2,256,4,128]{1,3,2,0:T(8,128)(2,1)} %get-tuple-element.108), channel_id=1, source_target_pairs={{25,31},{26,30},{27,29},{29,27},{30,26},{31,25}} | collective-permute-start | bytes 1572872 | tf_op jit(solution)/shard_map/ppermute | solution.py:78
  382.8 54.6 %collective-permute-start.36 = (bf16[2,256,4,128]{1,3,2,0:T(8,128)(2,1)S(1)}, bf16[2,256,4,128]{1,3,2,0:T(8,128)(2,1)S(1)}, u32[]{:S(2)}, u32[]{:S(2)}) collective-permute-start(bf16[2,256,4,128]{1,3,2,0:T(8,128)(2,1)S(1)} %copy-done), channel_id=1, source_target_pairs={{6,0},{7,1},{8,2},{9,3},{10,4},{11,5},{12,6},{13,7},{14,8},{15,9},... | collective-permute-start | bytes 1572872 | tf_op jit(solution)/shard_map/ppermute | solution.py:75
  406.4 41.4 %collective-permute-start.38 = (bf16[2,256,4,128]{1,3,2,0:T(8,128)(2,1)S(1)}, bf16[2,256,4,128]{1,3,2,0:T(8,128)(2,1)S(1)}, u32[]{:S(2)}, u32[]{:S(2)}) collective-permute-start(bf16[2,256,4,128]{1,3,2,0:T(8,128)(2,1)S(1)} %copy-done), channel_id=1, source_target_pairs={{5,0},{6,1},{7,2},{8,3},{9,4},{10,5},{11,6},{12,7},{13,8},{14,9},{... | collective-permute-start | bytes 1572872 | tf_op jit(solution)/shard_map/ppermute | solution.py:75
  447.8 44.3 %collective-permute-start.43 = (bf16[2,256,4,128]{1,3,2,0:T(8,128)(2,1)}, bf16[2,256,4,128]{1,3,2,0:T(8,128)(2,1)S(1)}, u32[]{:S(2)}, u32[]{:S(2)}) collective-permute-start(bf16[2,256,4,128]{1,3,2,0:T(8,128)(2,1)} %get-tuple-element.108), channel_id=1, source_target_pairs={{29,31},{31,29}} | collective-permute-start | bytes 1572872 | tf_op jit(solution)/shard_map/ppermute | solution.py:78
  450.7 50.6 %collective-permute-start.44 = (bf16[2,256,4,128]{1,3,2,0:T(8,128)(2,1)S(1)}, bf16[2,256,4,128]{1,3,2,0:T(8,128)(2,1)S(1)}, u32[]{:S(2)}, u32[]{:S(2)}) collective-permute-start(bf16[2,256,4,128]{1,3,2,0:T(8,128)(2,1)S(1)} %copy-done), channel_id=1, source_target_pairs={{2,0},{3,1},{4,2},{5,3},{6,4},{7,5},{8,6},{9,7},{10,8},{11,9},{12,... | collective-permute-start | bytes 1572872 | tf_op jit(solution)/shard_map/ppermute | solution.py:75
  461.1 40.2 %collective-permute-start.45 = (bf16[2,256,4,128]{1,3,2,0:T(8,128)(2,1)}, bf16[2,256,4,128]{1,3,2,0:T(8,128)(2,1)S(1)}, u32[]{:S(2)}, u32[]{:S(2)}) collective-permute-start(bf16[2,256,4,128]{1,3,2,0:T(8,128)(2,1)} %get-tuple-element.108), channel_id=1, source_target_pairs={{30,31},{31,30}} | collective-permute-start | bytes 1572872 | tf_op jit(solution)/shard_map/ppermute | solution.py:78
  (18 other events, 588.7 us)
where the time goes:
time: 688 us; the launch traced here: 686 us
  starting transfers between devices  326 us (47%)
  matrix products  146 us (21%)
  waiting for transfers between devices  97.4 us (14%)
  other arithmetic  67.1 us (10%)
  local copies, waits for them, and re-layouts  48 us (7%)
    ppermute x15, starting transfers between devices, device_step(): from_fold.append(lax.ppermute(kv_first, 'cp', fold_pairs))  122 us
    ppermute x16, starting transfers between devices, device_step(): lax.ppermute(kv_second, 'cp', [(sender, sender - offset) for sender in ra...  103 us
    ppermute x16, starting transfers between devices, device_step(): lax.ppermute(kv_first, 'cp', [(sender, sender + offset) for sender in ran...  101 us
    dot_general x2, matrix products, one_block(): jnp.einsum('nqkgd,nskd->nkgqs', q_part, k_part, preferred_element_type=jn...  55.9 us
    dot_general x2, matrix products, one_block(): jnp.einsum('nkgqs,nskd->nqkgd', exp_scores.astype(jnp.bfloat16), v_part,...  54.4 us
    reduce_sum x2, other arithmetic, one_block(): row_sum = jnp.sum(exp_scores, axis=-1)  43.5 us
    ppermute x16, waiting for transfers between devices, device_step(): lax.ppermute(kv_second, 'cp', [(sender, sender - offset) for sender in ra...  40.6 us
    unnamed x24, local copies, waits for them, and re-layouts  35.2 us
  transfers between devices with their start and end apart: 47, of which 10 were waited for; matrix products, arithmetic and copies ran while one was open for 9% of the time, Pallas kernels for 0%

commit v1 on v0

v1 whole, which is shorter than its diff:
```python
import functools
import math

import jax
import jax.numpy as jnp
from jax import lax
from jax.experimental import pallas as pl
from jax.experimental.pallas import tpu as pltpu
from jax.sharding import PartitionSpec as P

WINDOW = 4096
ROPE_BASE = 10000.0
NEG = -jnp.inf


def rotate(values, positions, factor):
    half_dim = values.shape[-1] // 2
    inv_freq = 1.0 / (ROPE_BASE ** (jnp.arange(half_dim, dtype=jnp.float32) * (2.0 / values.shape[-1])))
    angles = positions.astype(jnp.float32)[..., None, None] * inv_freq
    cos_part = jnp.cos(angles)
    sin_part = jnp.sin(angles)
    first_half = values[..., :half_dim].astype(jnp.float32)
    second_half = values[..., half_dim:].astype(jnp.float32)
    rotated = jnp.concatenate([first_half * cos_part - second_half * sin_part, second_half * cos_part + first_half * sin_part], axis=-1)
    return (rotated * factor).astype(jnp.bfloat16)


class Plan:
    def __init__(self, cp_size):
        self.chips = cp_size // 2
        self.row = math.isqrt(self.chips)
        self.span = 2 * self.row

    def pair(self, chip, side):
        return jnp.where(side == 0, chip, 2 * self.chips - 1 - chip)

    def chip_of(self, pair):
        return jnp.where(pair < self.chips, pair, 2 * self.chips - 1 - pair)

    def side_of(self, pair):
        return jnp.where(pair < self.chips, 0, 1)

    def twin(self, pair, slot):
        same = 2 * self.chip_of(pair) + slot - (2 * self.chips - 1)
        return jnp.where(pair < self.chips, -1, same)


def attention_kernel(plan, q_ref, kv_ref, out_ref, qbuf, kvbuf, acc, m_ref, l_ref, ostage, orecv,
                     loc_sem, pair_send, pair_recv, send_sem, recv_sem):
    me = lax.axis_index('cp')
    chip = me // 2
    core = lax.rem(me, 2)
    other = 1 - core
    row = plan.row
    x = lax.rem(chip, row)
    y = chip // row
    n_row = plan.chips // row
    chunk = qbuf.shape[4]
    heads_j = qbuf.shape[2]
    group = qbuf.shape[3]
    head_dim = qbuf.shape[5]
    half_cols = heads_j * group * head_dim

    def device(target_chip, target_core):
        return {'cp': target_chip * 2 + target_core}

    barrier = pltpu.get_barrier_semaphore()
    pl.semaphore_signal(barrier, inc=1, device_id=device(chip, other), device_id_type=pl.DeviceIdType.MESH)
    for step in range(1, row):
        mate = y * row + lax.rem(x + step, row)
        pl.semaphore_signal(barrier, inc=1, device_id=device(mate, core), device_id_type=pl.DeviceIdType.MESH)
    for dy in (-1, 1):
        @pl.when((y + dy >= 0) & (y + dy < n_row))
        def _():
            pl.semaphore_signal(barrier, inc=1, device_id=device(chip + dy * row, core), device_id_type=pl.DeviceIdType.MESH)
    pl.semaphore_wait(barrier, row + jnp.where(y > 0, 1, 0) + jnp.where(y < n_row - 1, 1, 0))

    partner = device(chip, other)
    pairs = [plan.pair(chip, s) for s in range(2)]
    own_sub = [core, other]

    pair_kv = []
    pair_q = []
    local = []
    for s in range(2):
        pair_kv.append(pltpu.make_async_remote_copy(
            src_ref=kv_ref.at[other, s], dst_ref=kvbuf.at[s, 0, own_sub[s]], send_sem=pair_send.at[s],
            recv_sem=pair_recv.at[s], device_id=partner, device_id_type=pl.DeviceIdType.MESH))
        pair_q.append(pltpu.make_async_remote_copy(
            src_ref=q_ref.at[other, s], dst_ref=qbuf.at[s, own_sub[s]], send_sem=pair_send.at[2 + s],
            recv_sem=pair_recv.at[2 + s], device_id=partner, device_id_type=pl.DeviceIdType.MESH))
        local.append(pltpu.make_async_copy(kv_ref.at[core, s], kvbuf.at[s, 0, own_sub[s]], loc_sem.at[s]))
        local.append(pltpu.make_async_copy(q_ref.at[core, s], qbuf.at[s, own_sub[s]], loc_sem.at[2 + s]))
    for copy in pair_kv + pair_q + local:
        copy.start()

    acc[...] = jnp.zeros_like(acc)
    l_ref[...] = jnp.zeros_like(l_ref)
    m_ref[...] = jnp.full_like(m_ref, NEG)

    def held(side, slot):
        twin = plan.twin(pairs[side], slot)
        return (jnp.where(twin >= 0, 0, side), jnp.where(twin >= 0, twin, slot))

    sent = []

    def send(side, slot, delta, cond):
        node = pairs[side] + delta
        goal = slot + delta
        ok = cond & (node < 2 * plan.chips) & (pairs[side] - slot >= 0) & (plan.twin(node, goal) < 0)
        held_side, held_slot = held(side, slot)
        index = len(sent)
        copy = pltpu.make_async_remote_copy(
            src_ref=kvbuf.at[held_side, held_slot], dst_ref=kvbuf.at[plan.side_of(node), goal],
            send_sem=send_sem.at[index], recv_sem=recv_sem.at[plan.side_of(node), goal],
            device_id=device(plan.chip_of(node), core), device_id_type=pl.DeviceIdType.MESH)
        sent.append((copy, ok))

        @pl.when(ok)
        def _():
            copy.start()

    def arrive(side, slot, extra=True):
        ok = (pairs[side] - slot >= 0) & (plan.twin(pairs[side], slot) < 0) & extra

        @pl.when(ok)
        def _():
            buf = kvbuf.at[side, slot]
            pltpu.make_async_remote_copy(
                src_ref=buf, dst_ref=buf, send_sem=send_sem.at[0], recv_sem=recv_sem.at[side, slot],
                device_id=partner, device_id_type=pl.DeviceIdType.MESH).wait_recv()

    def along(side, step):
        col = lax.rem(pairs[side], row)
        goal = lax.rem(col + step, row)
        return goal - col

    always = jnp.bool_(True)
    for copy in pair_kv:
        copy.wait_recv()
    for copy in local:
        copy.wait()
    for s in range(2):
        send(s, 0, row, always)
        for step in (1, row - 1) + tuple(range(2, row - 1)):
            delta = along(s, step)
            send(s, 0, delta, delta > 0)
    for copy in pair_q:
        copy.wait_recv()

    def block(side, slot_side, slot, j, a, masked, edge):
        k = kvbuf[slot_side, slot, :, 0, j].reshape(2 * chunk, head_dim)
        v = kvbuf[slot_side, slot, :, 1, j].reshape(2 * chunk, head_dim)
        scores = []
        for g in range(group):
            scores.append(lax.dot_general(qbuf[side, a, j, g], k, (((1,), (1,)), ((), ())), preferred_element_type=jnp.float32))
        if masked:
            rows = lax.broadcasted_iota(jnp.int32, (chunk, 2 * chunk), 0) + a * chunk
            cols = lax.broadcasted_iota(jnp.int32, (chunk, 2 * chunk), 1)
            allowed = (cols > rows) if edge else (cols <= rows)
        for g in range(group):
            s = scores[g]
            if masked:
                s = jnp.where(allowed, s, NEG)
            m_old = m_ref[side, a, j, g]
            m_new = jnp.maximum(m_old, jnp.max(s, axis=1, keepdims=True))
            alpha = jnp.exp(m_old - m_new)
            e = jnp.exp(s - jnp.concatenate([m_new] * (2 * chunk // m_new.shape[1]), axis=1))
            part = e[:, :head_dim]
            for b in range(1, 2 * chunk // head_dim):
                part = part + e[:, b * head_dim:(b + 1) * head_dim]
            m_ref[side, a, j, g] = m_new
            l_ref[side, a, j, g] = l_ref[side, a, j, g] * alpha + part
            acc[side, a, j, g] = acc[side, a, j, g] * alpha + jnp.dot(e.astype(jnp.bfloat16), v, preferred_element_type=jnp.float32)

    def sweep(side, slot, masked=False, edge=False):
        slot_side, at = held(side, slot) if isinstance(side, int) else (
            jnp.where(plan.twin(jnp.where(side == 0, pairs[0], pairs[1]), slot) >= 0, 0, side),
            jnp.where(plan.twin(jnp.where(side == 0, pairs[0], pairs[1]), slot) >= 0,
                      plan.twin(jnp.where(side == 0, pairs[0], pairs[1]), slot), slot))
        mine = jnp.where(side == 0, pairs[0], pairs[1])

        @pl.when(mine - slot >= 0)
        def _():
            def body(i, carry):
                block(side, slot_side, at, i // 2, lax.rem(i, 2), masked, edge)
                return carry
            lax.fori_loop(0, heads_j * 2, body, 0)

    lax.fori_loop(0, 2, lambda s, c: (sweep(s, 0, True, False), c)[1], 0)

    def hand_on(side, cond):
        for step in (1, row - 1) + tuple(range(2, row - 1)):
            delta = along(side, step)
            send(side, row, delta, cond & (delta < 0))
        send(side, row, row, cond)

    arrive(0, row)
    hand_on(0, always)
    arrive(1, row)
    single = plan.twin(pairs[1], row) < 0
    hand_on(1, single)
    sweep_full = lambda side, slot: sweep(side, slot)
    n_near = 2 * (row - 1)

    def near(i, carry):
        return carry

    for d in range(1, row):
        for s in range(2):
            arrive(s, d)
            send(s, d, row, always)
    hand_on(1, jnp.logical_not(single))
    def full(i, carry):
        late = i >= 2 * row
        k = jnp.where(late, i - 2 * row, i)
        slot = jnp.where(late, row + 1, 1) + k // 2
        side = lax.rem(k, 2)

        for d in range(row + 1, plan.span):
            for s in range(2):
                @pl.when(i == 2 * (d - 1) + s)
                def _():
                    arrive(s, d)
        sweep(side, slot)
        return carry

    lax.fori_loop(0, 2 * (plan.span - 1), full, 0)
    arrive(0, plan.span)
    arrive(1, plan.span)
    lax.fori_loop(0, 2, lambda s, c: (sweep(s, plan.span, True, True), c)[1], 0)

    first_col = pl.multiple_of(core * half_cols, half_cols)
    back_col = pl.multiple_of(core * half_cols, half_cols)

    def finish(i, carry):
        s = i // 2
        a = lax.rem(i, 2)
        mine = a == jnp.where(s == 0, core, other)
        for j in range(heads_j):
            for g in range(group):
                total = jnp.sum(l_ref[s, a, j, g], axis=1, keepdims=True)
                o = (acc[s, a, j, g] / total).astype(jnp.bfloat16)
                col = (j * group + g) * head_dim
                ostage[jnp.where(mine, 0, 1), s, :, col:col + head_dim] = o
        return carry

    lax.fori_loop(0, 4, finish, 0)
    back = pltpu.make_async_remote_copy(
        src_ref=ostage.at[1], dst_ref=orecv, send_sem=pair_send.at[4], recv_sem=pair_recv.at[4],
        device_id=partner, device_id_type=pl.DeviceIdType.MESH)
    back.start()
    other_col = pl.multiple_of(other * half_cols, half_cols)
    out_ref[:, :, pl.ds(first_col, half_cols)] = ostage[0]
    back.wait_recv()
    out_ref[:, :, pl.ds(other_col, half_cols)] = orecv[...]
    back.wait_send()
    for copy in pair_kv + pair_q:
        copy.wait_send()
    for copy, ok in sent:
        @pl.when(ok)
        def _():
            copy.wait_send()


def attend(plan, q_all, kv_all):
    _, _, heads_j, group, chunk, head_dim = q_all.shape
    bf16, f32 = jnp.bfloat16, jnp.float32
    slots = plan.span + 1
    n_send = 2 * (plan.row + 2 * plan.row + plan.row)
    return pl.pallas_call(
        functools.partial(attention_kernel, plan),
        out_shape=jax.ShapeDtypeStruct((2, chunk, 2 * heads_j * group * head_dim), bf16),
        in_specs=[pl.BlockSpec(memory_space=pltpu.VMEM)] * 2,
        out_specs=pl.BlockSpec(memory_space=pltpu.VMEM),
        scratch_shapes=[
            pltpu.VMEM((2, 2, heads_j, group, chunk, head_dim), bf16),
            pltpu.VMEM((2, slots, 2, 2, heads_j, chunk, head_dim), bf16),
            pltpu.VMEM((2, 2, heads_j, group, chunk, head_dim), f32),
            pltpu.VMEM((2, 2, heads_j, group, chunk, head_dim), f32),
            pltpu.VMEM((2, 2, heads_j, group, chunk, head_dim), f32),
            pltpu.VMEM((2, 2, chunk, heads_j * group * head_dim), bf16),
            pltpu.VMEM((2, chunk, heads_j * group * head_dim), bf16),
            pltpu.SemaphoreType.DMA((4,)),
            pltpu.SemaphoreType.DMA((5,)),
            pltpu.SemaphoreType.DMA((5,)),
            pltpu.SemaphoreType.DMA((64,)),
            pltpu.SemaphoreType.DMA((2, slots)),
        ],
        compiler_params=pltpu.CompilerParams(collective_id=0, has_side_effects=True, vmem_limit_bytes=56 * 1024 * 1024),
        name='attend',
    )(q_all, kv_all)


def solution(mesh):
    cp_size = mesh.shape['cp']
    plan = Plan(cp_size)

    def device_step(hidden, w_q, w_k, w_v, w_o):
        my_index = lax.axis_index('cp')
        chunk_len = hidden.shape[0] // 2
        model_dim = hidden.shape[1]
        heads, head_dim = w_q.shape[1], w_q.shape[2]
        kv_heads = w_k.shape[1]
        group_size = heads // kv_heads
        x_halves = hidden.reshape(2, chunk_len, model_dim)
        chunk_ids = jnp.stack([my_index, 2 * cp_size - 1 - my_index])
        positions = chunk_ids[:, None] * chunk_len + jnp.arange(chunk_len)[None, :]
        key_proj = jnp.einsum('nqd,dhe->nqhe', x_halves, w_k, preferred_element_type=jnp.float32).astype(jnp.bfloat16)
        val_proj = jnp.einsum('nqd,dhe->nqhe', x_halves, w_v, preferred_element_type=jnp.float32).astype(jnp.bfloat16)
        kv = jnp.stack([rotate(key_proj, positions, 1.0), val_proj], axis=1)
        kv_all = kv.reshape(2, 2, chunk_len, 2, kv_heads // 2, head_dim).transpose(3, 0, 1, 4, 2, 5)
        q_proj = jnp.einsum('nqd,dhe->nqhe', x_halves, w_q, preferred_element_type=jnp.float32).astype(jnp.bfloat16)
        queries = rotate(q_proj, positions, head_dim ** -0.5)
        q_all = queries.reshape(2, chunk_len, 2, kv_heads // 2, group_size, head_dim).transpose(2, 0, 3, 4, 1, 5)
        attended = attend(plan, q_all, kv_all)
        out_rows = jnp.dot(attended.reshape(2 * chunk_len, heads * head_dim), w_o.reshape(heads * head_dim, model_dim), preferred_element_type=jnp.float32)
        return out_rows.astype(jnp.bfloat16)

    return jax.shard_map(device_step, mesh=mesh, in_specs=(P(('dp', 'cp'), None), P(), P(), P(), P()), out_specs=P(('dp', 'cp'), None), check_vma=False)
```

time: 688 us -> 218 us (0.32)
  the two profiles are of different devices: /device:TPU:125 before, /device:TPU:123 now
where the time goes in v1:
time: 218 us; the launch traced here: 216 us
  Pallas kernels  130 us (60%)
  matrix products  39.6 us (18%)
  local copies, waits for them, and re-layouts  36.5 us (17%)
  other arithmetic  10.1 us (5%)
    pallas_call x1, Pallas kernels, attend(): pl.pallas_call(functools.partial(attention_kernel, plan), out_shape=jax.S...  130 us
    unnamed x2, local copies, waits for them, and re-layouts  29.4 us
    dot_general x1, matrix products, device_step(): jnp.dot(attended.reshape(2 * chunk_len, heads * head_dim), w_o.reshape(he...  14.3 us
    dot_general x1, matrix products, device_step(): jnp.einsum('nqd,dhe->nqhe', x_halves, w_q, preferred_element_type=jnp.flo...  13.7 us
    concatenate x4, local copies, waits for them, and re-layouts, rotate(): jnp.concatenate([first_half * cos_part - second_half * sin_part, second_h...  7.09 us
    transpose x1, other arithmetic, device_step(): queries.reshape(2, chunk_len, 2, kv_heads // 2, group_size, head_dim)  5.93 us
    dot_general x1, matrix products, device_step(): jnp.einsum('nqd,dhe->nqhe', x_halves, w_k, preferred_element_type=jnp.flo...  5.82 us
    dot_general x1, matrix products, device_step(): jnp.einsum('nqd,dhe->nqhe', x_halves, w_v, preferred_element_type=jnp.flo...  5.8 us

profile of v1, /device:TPU:123, one launch (start us, length us, event | category | flops | bytes accessed | tf_op | source)
XLA Modules:
  0.0 216.0 jit_solution(8651370731361216728)
XLA Ops:
  0.0 0.1 add_multiply_fusion
  0.1 0.1 add_convert_fusion
  0.2 0.5 multiply_cosine_fusion
  0.7 22.0 %copy.9 = bf16[4096,16,128]{0,2,1:T(8,128)(2,1)} copy(bf16[4096,16,128]{2,1,0:T(8,128)(2,1)} %param.6) | data formatting | bytes 33554432 | tf_op args[1]
  22.7 13.7 %fusion.11 = bf16[2,256,16,128]{1,3,2,0:T(8,128)(2,1)S(1)} fusion(bf16[2,256,4096,1]{2,1,3,0:T(8,128)(2,1)} %bitcast.45, bf16[4096,16,128]{0,2,1:T(8,128)(2,1)} %copy.9), kind=kOutput, calls=%fused_computation.17 | convolution fusion | flops 8590983168 | bytes 23068672 | tf_op jit(solution)/shard_map/nqd,dhe->nqhe/dot_general | solution.py:313
  36.4 2.0 fusion.8
  38.4 3.8 %copy.11 = f32[2,256,2,2,4,64]{5,1,4,3,0,2:T(8,128)} copy(f32[2,256,2,2,4,64]{1,5,4,3,2,0:T(8,128)} %bitcast.39) | data formatting | bytes 4194304 | tf_op jit(solution)/shard_map/concatenate | solution.py:24
  42.2 2.7 %copy.10 = f32[2,256,2,2,4,64]{5,1,4,3,0,2:T(8,128)} copy(f32[2,256,2,2,4,64]{1,5,4,3,2,0:T(8,128)S(1)} %bitcast.38) | data formatting | bytes 4194304 | tf_op jit(solution)/shard_map/concatenate | solution.py:24
  44.9 5.9 %fusion.10.q_ref = bf16[2,2,2,4,256,128]{5,4,3,2,1,0:T(8,128)(2,1)} fusion(f32[2,256,2,2,4,64]{5,1,4,3,0,2:T(8,128)} %copy.11, f32[2,256,2,2,4,64]{5,1,4,3,0,2:T(8,128)} %copy.10), kind=kLoop, calls=%fused_computation.16 | loop fusion | flops 3145728 | bytes 6291456 | tf_op jit(solution)/shard_map/transpose | solution.py:315
  50.9 7.4 %copy.12 = bf16[4096,4,128]{0,2,1:T(8,128)(2,1)} copy(bf16[4096,4,128]{2,1,0:T(4,128)(2,1)} %param.7) | data formatting | bytes 8388608 | tf_op args[2]
  58.3 5.8 %fusion.14 = bf16[2,256,4,128]{1,3,2,0:T(8,128)(2,1)S(1)} fusion(bf16[2,256,4096,1]{2,1,3,0:T(8,128)(2,1)} %bitcast.46, bf16[4096,4,128]{0,2,1:T(8,128)(2,1)} %copy.12), kind=kOutput, calls=%fused_computation.18 | convolution fusion | flops 2147745792 | bytes 8912896 | tf_op jit(solution)/shard_map/nqd,dhe->nqhe/dot_general | solution.py:309
  64.1 0.2 fusion.21
  64.3 0.3 copy.14
  64.6 0.3 copy.13
  64.9 5.8 %fusion.17 = bf16[2,256,4,128]{3,1,2,0:T(8,128)(2,1)S(1)} fusion(bf16[2,256,4096,1]{2,1,3,0:T(8,128)(2,1)} %bitcast.47, bf16[4096,4,128]{2,1,0:T(4,128)(2,1)} %param.8), kind=kOutput, calls=%fused_computation.19 | convolution fusion | flops 2147745792 | bytes 8912896 | tf_op jit(solution)/shard_map/nqd,dhe->nqhe/dot_general | solution.py:310
  70.7 1.3 maximum_bitcast_fusion.kv_ref
  72.0 129.8 %attend.1 = bf16[2,256,2048]{2,1,0:T(8,128)(2,1)} custom-call(bf16[2,2,2,4,256,128]{5,4,3,2,1,0:T(8,128)(2,1)} %fusion.10.q_ref, bf16[2,2,2,2,256,128]{5,4,3,2,1,0:T(8,128)(2,1)} %maximum_bitcast_fusion.kv_ref), custom_call_target="tpu_custom_call" | custom-call | tf_op jit(solution)/shard_map/attend/pallas_call | solution.py:271
  201.7 14.3 %convolution_convert_fusion = bf16[512,4096]{1,0:T(8,128)(2,1)} fusion(bf16[512,2048]{1,0:T(8,128)(2,1)} %bitcast.40, bf16[2048,4096]{1,0:T(8,128)(2,1)} %bitcast.44), kind=kOutput, calls=%fused_computation.2 | convolution fusion | flops 8592031744 | bytes 23068672 | tf_op jit(solution)/shard_map/dot_general | solution.py:317
  (1 shorter events, 0.0 us)

commit v2 on v1

--- a/solution.py
+++ b/solution.py
@@ -13,16 +13,99 @@
 NEG = -jnp.inf
 
 
-def rotate(values, positions, factor):
-    half_dim = values.shape[-1] // 2
-    inv_freq = 1.0 / (ROPE_BASE ** (jnp.arange(half_dim, dtype=jnp.float32) * (2.0 / values.shape[-1])))
-    angles = positions.astype(jnp.float32)[..., None, None] * inv_freq
+def rotary_tables(positions, head_dim):
+    half_dim = head_dim // 2
+    inv_freq = 1.0 / (ROPE_BASE ** (jnp.arange(half_dim, dtype=jnp.float32) * (2.0 / head_dim)))
+    angles = positions.astype(jnp.float32)[:, None] * inv_freq
     cos_part = jnp.cos(angles)
     sin_part = jnp.sin(angles)
-    first_half = values[..., :half_dim].astype(jnp.float32)
-    second_half = values[..., half_dim:].astype(jnp.float32)
-    rotated = jnp.concatenate([first_half * cos_part - second_half * sin_part, second_half * cos_part + first_half * sin_part], axis=-1)
-    return (rotated * factor).astype(jnp.bfloat16)
+    return jnp.concatenate([cos_part, cos_part], axis=-1), jnp.concatenate([-sin_part, sin_part], axis=-1)
+
+
+def spread(n_heads, size):
+    per = size // n_heads
+    to = lax.broadcasted_iota(jnp.int32, (size, size), 0)
+    of = lax.broadcasted_iota(jnp.int32, (size, size), 1)
+    return jnp.where((to % per) * n_heads + to // per == of, 1.0, 0.0).astype(jnp.bfloat16)
+
+
+def by_head(mix, rows_ref, start, dst_ref, n_heads):
+    size = mix.shape[0]
+    per = size // n_heads
+    wide = jnp.concatenate([rows_ref[pl.ds(start, size)], rows_ref[pl.ds(pl.multiple_of(start + size, size), size)]], axis=1)
+    head_dim = wide.shape[1] // 2
+    out = jnp.dot(mix, wide, preferred_element_type=jnp.float32).astype(jnp.bfloat16)
+    at = pl.multiple_of(start // n_heads, 2 * per)
+    for b in range(2):
+        for h in range(n_heads):
+            dst_ref[pl.ds(pl.multiple_of(at + b * per, per), per), h * head_dim:(h + 1) * head_dim] = out[h * per:(h + 1) * per, b * head_dim:(b + 1) * head_dim]
+
+
+MIX = 256
+
+
+def kv_kernel(n_heads, x_ref, wk_ref, wv_ref, cos_ref, sin_ref, out_ref, mix, wk, wv, acc_k, acc_v):
+    step = pl.program_id(0)
+
+    @pl.when(step == 0)
+    def _():
+        mix[...] = spread(n_heads, MIX)
+        acc_k[...] = jnp.zeros_like(acc_k)
+        acc_v[...] = jnp.zeros_like(acc_v)
+
+    def arrange(i, carry):
+        start = pl.multiple_of(i * (2 * MIX), 2 * MIX)
+        by_head(mix[...], wk_ref, start, wk, n_heads)
+        by_head(mix[...], wv_ref, start, wv, n_heads)
+        return carry
+
+    lax.fori_loop(0, wk_ref.shape[0] // (2 * MIX), arrange, 0, unroll=2)
+    acc_k[...] += jnp.dot(x_ref[...], wk[...], preferred_element_type=jnp.float32)
+    acc_v[...] += jnp.dot(x_ref[...], wv[...], preferred_element_type=jnp.float32)
+
+    @pl.when(step == pl.num_programs(0) - 1)
+    def _():
+        chunk, head_dim = out_ref.shape[4], out_ref.shape[5]
+        half = n_heads // 2
+        for n in range(2):
+            rows = slice(n * chunk, (n + 1) * chunk)
+            for h in range(n_heads):
+                cols = slice(h * head_dim, (h + 1) * head_dim)
+                k = acc_k[rows, cols].astype(jnp.bfloat16).astype(jnp.float32)
+                k = k * cos_ref[rows] + pltpu.roll(k, head_dim // 2, 1) * sin_ref[rows]
+                out_ref[h // half, n, 0, h % half] = k.astype(jnp.bfloat16)
+                out_ref[h // half, n, 1, h % half] = acc_v[rows, cols].astype(jnp.bfloat16)
+
+
+def project_kv(hidden, w_k, w_v, cos, sin):
+    rows, model_dim = hidden.shape
+    n_heads, head_dim = w_k.shape[1:]
+    chunk = rows // 2
+    depth = model_dim // 4
+    bf16, f32 = jnp.bfloat16, jnp.float32
+    cols = n_heads * head_dim
+    return pl.pallas_call(
+        functools.partial(kv_kernel, n_heads),
+        grid=(model_dim // depth,),
+        in_specs=[
+            pl.BlockSpec((rows, depth), lambda i: (0, i)),
+            pl.BlockSpec((depth * n_heads, head_dim), lambda i: (i, 0)),
+            pl.BlockSpec((depth * n_heads, head_dim), lambda i: (i, 0)),
+            pl.BlockSpec((rows, head_dim), lambda i: (0, 0)),
+            pl.BlockSpec((rows, head_dim), lambda i: (0, 0)),
+        ],
+        out_specs=pl.BlockSpec((2, 2, 2, n_heads // 2, chunk, head_dim), lambda i: (0, 0, 0, 0, 0, 0)),
+        out_shape=jax.ShapeDtypeStruct((2, 2, 2, n_heads // 2, chunk, head_dim), bf16),
+        scratch_shapes=[
+            pltpu.VMEM((MIX, MIX), bf16),
+            pltpu.VMEM((depth, cols), bf16),
+            pltpu.VMEM((depth, cols), bf16),
+            pltpu.VMEM((rows, cols), f32),
+            pltpu.VMEM((rows, cols), f32),
+        ],
+        compiler_params=pltpu.CompilerParams(dimension_semantics=('arbitrary',), vmem_limit_bytes=40 * 1024 * 1024),
+        name='project_kv',
+    )(hidden, w_k.reshape(model_dim * n_heads, head_dim), w_v.reshape(model_dim * n_heads, head_dim), cos, sin)
 
 
 class Plan:
@@ -45,8 +128,8 @@
         return jnp.where(pair < self.chips, -1, same)
 
 
-def attention_kernel(plan, q_ref, kv_ref, out_ref, qbuf, kvbuf, acc, m_ref, l_ref, ostage, orecv,
-                     loc_sem, pair_send, pair_recv, send_sem, recv_sem):
+def attention_kernel(plan, x_ref, wq_ref, cos_ref, sin_ref, kv_ref, out_ref, qbuf, qstage, kvbuf, acc, m_ref, l_ref,
+                     ostage, orecv, mix, wraw, wsort, accq, loc_sem, w_sem, pair_send, pair_recv, send_sem, recv_sem):
     me = lax.axis_index('cp')
     chip = me // 2
     core = lax.rem(me, 2)
@@ -79,6 +162,18 @@
     pairs = [plan.pair(chip, s) for s in range(2)]
     own_sub = [core, other]
 
+    n_heads = 2 * heads_j * group
+    depth = wsort.shape[0]
+    raw_rows = depth * n_heads
+    n_blocks = wq_ref.shape[0] // raw_rows
+
+    def fetch(block):
+        at = pl.multiple_of(block * raw_rows, raw_rows)
+        slot = lax.rem(block, 2)
+        return pltpu.make_async_copy(wq_ref.at[pl.ds(at, raw_rows)], wraw.at[slot], w_sem.at[slot])
+
+    fetch(0).start()
+
     pair_kv = []
     pair_q = []
     local = []
@@ -87,11 +182,10 @@
             src_ref=kv_ref.at[other, s], dst_ref=kvbuf.at[s, 0, own_sub[s]], send_sem=pair_send.at[s],
             recv_sem=pair_recv.at[s], device_id=partner, device_id_type=pl.DeviceIdType.MESH))
         pair_q.append(pltpu.make_async_remote_copy(
-            src_ref=q_ref.at[other, s], dst_ref=qbuf.at[s, own_sub[s]], send_sem=pair_send.at[2 + s],
+            src_ref=qstage.at[s], dst_ref=qbuf.at[s, own_sub[s]], send_sem=pair_send.at[2 + s],
             recv_sem=pair_recv.at[2 + s], device_id=partner, device_id_type=pl.DeviceIdType.MESH))
         local.append(pltpu.make_async_copy(kv_ref.at[core, s], kvbuf.at[s, 0, own_sub[s]], loc_sem.at[s]))
-        local.append(pltpu.make_async_copy(q_ref.at[core, s], qbuf.at[s, own_sub[s]], loc_sem.at[2 + s]))
-    for copy in pair_kv + pair_q + local:
+    for copy in pair_kv + local:
         copy.start()
 
     acc[...] = jnp.zeros_like(acc)
@@ -104,17 +198,26 @@
 
     sent = []
 
-    def send(side, slot, delta, cond):
+    def along(side, step):
+        col = lax.rem(pairs[side], row)
+        return lax.rem(col + step, row) - col
+
+    def describe(index, side, slot, where, cond):
+        delta = where()
         node = pairs[side] + delta
         goal = slot + delta
-        ok = cond & (node < 2 * plan.chips) & (pairs[side] - slot >= 0) & (plan.twin(node, goal) < 0)
+        ok = (node < 2 * plan.chips) & (pairs[side] - slot >= 0) & (plan.twin(node, goal) < 0) & cond()
         held_side, held_slot = held(side, slot)
-        index = len(sent)
         copy = pltpu.make_async_remote_copy(
             src_ref=kvbuf.at[held_side, held_slot], dst_ref=kvbuf.at[plan.side_of(node), goal],
             send_sem=send_sem.at[index], recv_sem=recv_sem.at[plan.side_of(node), goal],
             device_id=device(plan.chip_of(node), core), device_id_type=pl.DeviceIdType.MESH)
-        sent.append((copy, ok))
+        return copy, ok
+
+    def send(side, slot, where, cond):
+        spec = (len(sent), side, slot, where, cond)
+        sent.append(spec)
+        copy, ok = describe(*spec)
 
         @pl.when(ok)
         def _():
@@ -130,21 +233,71 @@
                 src_ref=buf, dst_ref=buf, send_sem=send_sem.at[0], recv_sem=recv_sem.at[side, slot],
                 device_id=partner, device_id_type=pl.DeviceIdType.MESH).wait_recv()
 
-    def along(side, step):
-        col = lax.rem(pairs[side], row)
-        goal = lax.rem(col + step, row)
-        return goal - col
-
-    always = jnp.bool_(True)
+    def always():
+        return pairs[0] >= 0
+
+    def down():
+        return row
+
     for copy in pair_kv:
         copy.wait_recv()
     for copy in local:
         copy.wait()
     for s in range(2):
-        send(s, 0, row, always)
-        for step in (1, row - 1) + tuple(range(2, row - 1)):
-            delta = along(s, step)
-            send(s, 0, delta, delta > 0)
+        send(s, 0, down, always)
+    for step in (1, row - 1):
+        for s in range(2):
+            where = functools.partial(along, s, step)
+            send(s, 0, where, lambda w=where: w() > 0)
+
+    mix[...] = spread(n_heads, MIX)
+    accq[...] = jnp.zeros_like(accq)
+
+    def project(block, carry):
+        fetch(block).wait()
+
+        @pl.when(block + 1 < n_blocks)
+        def _():
+            fetch(block + 1).start()
+
+        raw = wraw.at[lax.rem(block, 2)]
+
+        def arrange(i, c):
+            by_head(mix[...], raw, pl.multiple_of(i * (2 * MIX), 2 * MIX), wsort, n_heads)
+            return c
+
+        lax.fori_loop(0, raw_rows // (2 * MIX), arrange, 0, unroll=4)
+        at = pl.multiple_of(block * depth, depth)
+        accq[...] += jnp.dot(x_ref[:, pl.ds(at, depth)], wsort[...], preferred_element_type=jnp.float32)
+        return carry
+
+    lax.fori_loop(0, n_blocks, project, 0)
+
+    def turn(s, half, put):
+        rows = pl.ds(pl.multiple_of(s * chunk, chunk), chunk)
+        for j in range(heads_j):
+            for g in range(group):
+                col = pl.multiple_of(half * half_cols, half_cols) + (j * group + g) * head_dim
+                q = accq[rows, pl.ds(pl.multiple_of(col, head_dim), head_dim)].astype(jnp.bfloat16).astype(jnp.float32)
+                q = q * cos_ref[rows] + pltpu.roll(q, head_dim // 2, 1) * sin_ref[rows]
+                put(j, g, (q * head_dim ** -0.5).astype(jnp.bfloat16))
+
+    def for_partner(s, carry):
+        def put(j, g, q):
+            qstage[s, j, g] = q
+        turn(s, other, put)
+        return carry
+
+    def for_me(s, carry):
+        def put(j, g, q):
+            qbuf[s, jnp.where(s == 0, core, other), j, g] = q
+        turn(s, core, put)
+        return carry
+
+    lax.fori_loop(0, 2, for_partner, 0)
+    lax.fori_loop(0, 2, for_me, 0)
+    for copy in pair_q:
+        copy.start()
     for copy in pair_q:
         copy.wait_recv()
 
@@ -190,45 +343,71 @@
     lax.fori_loop(0, 2, lambda s, c: (sweep(s, 0, True, False), c)[1], 0)
 
     def hand_on(side, cond):
-        for step in (1, row - 1) + tuple(range(2, row - 1)):
-            delta = along(side, step)
-            send(side, row, delta, cond & (delta < 0))
-        send(side, row, row, cond)
-
-    arrive(0, row)
-    hand_on(0, always)
-    arrive(1, row)
-    single = plan.twin(pairs[1], row) < 0
-    hand_on(1, single)
-    sweep_full = lambda side, slot: sweep(side, slot)
-    n_near = 2 * (row - 1)
-
-    def near(i, carry):
+        for step in (1, row - 1):
+            where = functools.partial(along, side, step)
+            send(side, row, where, lambda w=where: cond() & (w() < 0))
+        send(side, row, down, cond)
+
+    def single():
+        return plan.twin(pairs[1], row) < 0
+
+    def double():
+        return plan.twin(pairs[1], row) >= 0
+
+    near, far = 1, row - 1
+
+    def pass_on(side, slot):
+        def inner():
+            col = lax.rem(pairs[side], row)
+            return (col > 0) & (col < row - 1)
+
+        send(side, slot, down, always)
+        if slot == near:
+            send(side, slot, lambda: 1, inner)
+        if slot == far:
+            send(side, slot, lambda: -1, inner)
+
+    def come(side, slot):
+        def event():
+            arrive(side, slot)
+            if slot < row:
+                pass_on(side, slot)
+        return event
+
+    def first():
+        arrive(0, row)
+        hand_on(0, always)
+        arrive(1, row)
+        hand_on(1, single)
+
+    order = [
+        (0, 4, first), (0, 1, come(0, 1)), (1, 1, come(1, 1)), (0, 3, come(0, 3)), (0, 2, come(0, 2)), (1, 3, come(1, 3)),
+        (1, 2, come(1, 2)), (1, 4, lambda: hand_on(1, double)),
+        (0, 8, come(0, 8)), (0, 5, come(0, 5)), (1, 5, come(1, 5)), (0, 7, come(0, 7)), (1, 8, come(1, 8)),
+        (0, 6, come(0, 6)), (1, 6, come(1, 6)), (1, 7, come(1, 7)),
+    ]
+
+    def visit(i, carry):
+        side = jnp.int32(0)
+        slot = jnp.int32(0)
+        for n, (s, d, event) in enumerate(order):
+            side = jnp.where(i == n, s, side)
+            slot = jnp.where(i == n, d, slot)
+
+            @pl.when(i == n)
+            def _():
+                event()
+
+        @pl.when(slot < plan.span)
+        def _():
+            sweep(side, slot)
+
+        @pl.when(slot == plan.span)
+        def _():
+            sweep(side, slot, True, True)
         return carry
 
-    for d in range(1, row):
-        for s in range(2):
-            arrive(s, d)
-            send(s, d, row, always)
-    hand_on(1, jnp.logical_not(single))
-    def full(i, carry):
-        late = i >= 2 * row
-        k = jnp.where(late, i - 2 * row, i)
-        slot = jnp.where(late, row + 1, 1) + k // 2
-        side = lax.rem(k, 2)
-
-        for d in range(row + 1, plan.span):
-            for s in range(2):
-                @pl.when(i == 2 * (d - 1) + s)
-                def _():
-                    arrive(s, d)
-        sweep(side, slot)
-        return carry
-
-    lax.fori_loop(0, 2 * (plan.span - 1), full, 0)
-    arrive(0, plan.span)
-    arrive(1, plan.span)
-    lax.fori_loop(0, 2, lambda s, c: (sweep(s, plan.span, True, True), c)[1], 0)
+    lax.fori_loop(0, len(order), visit, 0)
 
     first_col = pl.multiple_of(core * half_cols, half_cols)
     back_col = pl.multiple_of(core * half_cols, half_cols)
@@ -257,39 +436,50 @@
     back.wait_send()
     for copy in pair_kv + pair_q:
         copy.wait_send()
-    for copy, ok in sent:
+    for spec in sent:
+        copy, ok = describe(*spec)
+
         @pl.when(ok)
         def _():
             copy.wait_send()
 
 
-def attend(plan, q_all, kv_all):
-    _, _, heads_j, group, chunk, head_dim = q_all.shape
+def attend(plan, hidden, w_q, cos, sin, kv_all):
+    model_dim, heads, head_dim = w_q.shape
+    _, _, _, heads_j, chunk, _ = kv_all.shape
+    group = heads // (2 * heads_j)
     bf16, f32 = jnp.bfloat16, jnp.float32
     slots = plan.span + 1
-    n_send = 2 * (plan.row + 2 * plan.row + plan.row)
+    depth = model_dim // 8
+    vmem = pl.BlockSpec(memory_space=pltpu.VMEM)
     return pl.pallas_call(
         functools.partial(attention_kernel, plan),
-        out_shape=jax.ShapeDtypeStruct((2, chunk, 2 * heads_j * group * head_dim), bf16),
-        in_specs=[pl.BlockSpec(memory_space=pltpu.VMEM)] * 2,
-        out_specs=pl.BlockSpec(memory_space=pltpu.VMEM),
+        out_shape=jax.ShapeDtypeStruct((2, chunk, heads * head_dim), bf16),
+        in_specs=[vmem, pl.BlockSpec(memory_space=pl.ANY), vmem, vmem, vmem],
+        out_specs=vmem,
         scratch_shapes=[
             pltpu.VMEM((2, 2, heads_j, group, chunk, head_dim), bf16),
+            pltpu.VMEM((2, heads_j, group, chunk, head_dim), bf16),
             pltpu.VMEM((2, slots, 2, 2, heads_j, chunk, head_dim), bf16),
             pltpu.VMEM((2, 2, heads_j, group, chunk, head_dim), f32),
             pltpu.VMEM((2, 2, heads_j, group, chunk, head_dim), f32),
             pltpu.VMEM((2, 2, heads_j, group, chunk, head_dim), f32),
             pltpu.VMEM((2, 2, chunk, heads_j * group * head_dim), bf16),
             pltpu.VMEM((2, chunk, heads_j * group * head_dim), bf16),
-            pltpu.SemaphoreType.DMA((4,)),
+            pltpu.VMEM((MIX, MIX), bf16),
+            pltpu.VMEM((2, depth * heads, head_dim), bf16),
+            pltpu.VMEM((depth, heads * head_dim), bf16),
+            pltpu.VMEM((2 * chunk, heads * head_dim), f32),
+            pltpu.SemaphoreType.DMA((2,)),
+            pltpu.SemaphoreType.DMA((2,)),
             pltpu.SemaphoreType.DMA((5,)),
             pltpu.SemaphoreType.DMA((5,)),
             pltpu.SemaphoreType.DMA((64,)),
             pltpu.SemaphoreType.DMA((2, slots)),
         ],
-        compiler_params=pltpu.CompilerParams(collective_id=0, has_side_effects=True, vmem_limit_bytes=56 * 1024 * 1024),
+        compiler_params=pltpu.CompilerParams(collective_id=0, has_side_effects=True, vmem_limit_bytes=60 * 1024 * 1024),
         name='attend',
-    )(q_all, kv_all)
+    )(hidden, w_q.reshape(model_dim * heads, head_dim), cos, sin, kv_all)
 
 
 def solution(mesh):
@@ -301,19 +491,11 @@
         chunk_len = hidden.shape[0] // 2
         model_dim = hidden.shape[1]
         heads, head_dim = w_q.shape[1], w_q.shape[2]
-        kv_heads = w_k.shape[1]
-        group_size = heads // kv_heads
-        x_halves = hidden.reshape(2, chunk_len, model_dim)
         chunk_ids = jnp.stack([my_index, 2 * cp_size - 1 - my_index])
-        positions = chunk_ids[:, None] * chunk_len + jnp.arange(chunk_len)[None, :]
-        key_proj = jnp.einsum('nqd,dhe->nqhe', x_halves, w_k, preferred_element_type=jnp.float32).astype(jnp.bfloat16)
-        val_proj = jnp.einsum('nqd,dhe->nqhe', x_halves, w_v, preferred_element_type=jnp.float32).astype(jnp.bfloat16)
-        kv = jnp.stack([rotate(key_proj, positions, 1.0), val_proj], axis=1)
-        kv_all = kv.reshape(2, 2, chunk_len, 2, kv_heads // 2, head_dim).transpose(3, 0, 1, 4, 2, 5)
-        q_proj = jnp.einsum('nqd,dhe->nqhe', x_halves, w_q, preferred_element_type=jnp.float32).astype(jnp.bfloat16)
-        queries = rotate(q_proj, positions, head_dim ** -0.5)
-        q_all = queries.reshape(2, chunk_len, 2, kv_heads // 2, group_size, head_dim).transpose(2, 0, 3, 4, 1, 5)
-        attended = attend(plan, q_all, kv_all)
+        positions = (chunk_ids[:, None] * chunk_len + jnp.arange(chunk_len)[None, :]).reshape(2 * chunk_len)
+        cos, sin = rotary_tables(positions, head_dim)
+        kv_all = project_kv(hidden, w_k, w_v, cos, sin)
+        attended = attend(plan, hidden, w_q, cos, sin, kv_all)
         out_rows = jnp.dot(attended.reshape(2 * chunk_len, heads * head_dim), w_o.reshape(heads * head_dim, model_dim), preferred_element_type=jnp.float32)
         return out_rows.astype(jnp.bfloat16)
 

time: 218 us -> 170 us (0.78)
  the two profiles are of different devices: /device:TPU:123 before, /device:TPU:117 now
where the time goes in v2:
time: 170 us
  Pallas kernels  147 us (86%)
  matrix products  14.3 us (8%)
  local copies, waits for them, and re-layouts  7.72 us (5%)
    pallas_call x1, Pallas kernels, attend(): pl.pallas_call(functools.partial(attention_kernel, plan), out_shape=jax.S...  136 us
    dot_general x1, matrix products, device_step(): jnp.dot(attended.reshape(2 * chunk_len, heads * head_dim), w_o.reshape(he...  14.3 us
    pallas_call x1, Pallas kernels, project_kv(): pl.pallas_call(functools.partial(kv_kernel, n_heads), grid=(model_dim //...  11 us
    unnamed x13, local copies, waits for them, and re-layouts  7.72 us

profile of v2, /device:TPU:117, one launch (start us, length us, event | category | flops | bytes accessed | tf_op | source)
XLA Modules:
  0.0 170.0 jit_solution(14570563541051587535)
XLA Ops:
  0.0 0.1 add_multiply_fusion
  0.1 0.1 convert_bitcast_fusion
  0.2 1.0 fusion
  1.2 0.2 pad_maximum_fusion
  1.4 0.0 copy-start.4
  1.4 0.0 copy-start.5
  1.4 0.0 copy-start
  1.4 2.4 %copy-done = bf16[512,4096]{1,0:T(8,128)(2,1)S(1)} copy-done((bf16[512,4096]{1,0:T(8,128)(2,1)S(1)}, bf16[512,4096]{1,0:T(8,128)(2,1)}, u32[]{:S(2)}) %copy-start) | copy-done | bytes 4194328
  3.8 0.0 copy-start.1
  3.8 2.2 %copy-done.1 = bf16[4096,4,128]{2,1,0:T(4,128)(2,1)S(1)} copy-done((bf16[4096,4,128]{2,1,0:T(4,128)(2,1)S(1)}, bf16[4096,4,128]{2,1,0:T(4,128)(2,1)}, u32[]{:S(2)}) %copy-start.1) | copy-done | bytes 4194328
  6.0 0.0 copy-start.2
  6.0 2.2 %copy-done.2 = bf16[4096,4,128]{2,1,0:T(4,128)(2,1)S(1)} copy-done((bf16[4096,4,128]{2,1,0:T(4,128)(2,1)S(1)}, bf16[4096,4,128]{2,1,0:T(4,128)(2,1)}, u32[]{:S(2)}) %copy-start.2) | copy-done | bytes 4194328
  8.2 11.0 %project_kv.1.kv_ref = bf16[2,2,2,2,256,128]{5,4,3,2,1,0:T(8,128)(2,1)S(1)} custom-call(bf16[512,4096]{1,0:T(8,128)(2,1)S(1)} %copy-done, bf16[16384,128]{1,0:T(8,128)(2,1)S(1)} %bitcast.12, bf16[16384,128]{1,0:T(8,128)(2,1)S(1)} %bitcast.13, f32[512,128]{1,0:T(8,128)S(1)} %get-tuple-element.8.cos_ref, f32[512,128]{1,0:T(8,128)S(1)} %get-tuple-element.9.sin_ref), custom_call_target="tpu_custom_call" | custom-call | tf_op jit(solution)/shard_map/project_kv/pallas_call | solution.py:87
  19.2 0.0 copy-done.4
  19.2 0.0 copy-done.5
  19.2 0.0 copy-start.3
  19.2 1.0 copy-done.3
  20.1 135.5 %attend.1 = bf16[2,256,2048]{2,1,0:T(8,128)(2,1)} custom-call(bf16[512,4096]{1,0:T(8,128)(2,1)} %x_ref.3, bf16[65536,128]{1,0:T(8,128)(2,1)} %bitcast.14, f32[512,128]{1,0:T(8,128)} %copy-done.4, f32[512,128]{1,0:T(8,128)} %copy-done.5, bf16[2,2,2,2,256,128]{5,4,3,2,1,0:T(8,128)(2,1)} %copy-done.3), custom_call_target="tpu_custom_call" | custom-call | tf_op jit(solution)/shard_map/attend/pallas_call | solution.py:455
  155.7 14.3 %convolution_convert_fusion = bf16[512,4096]{1,0:T(8,128)(2,1)} fusion(bf16[512,2048]{1,0:T(8,128)(2,1)} %bitcast.15, bf16[2048,4096]{1,0:T(8,128)(2,1)} %bitcast.17), kind=kOutput, calls=%fused_computation | convolution fusion | flops 8592031744 | bytes 23068672 | tf_op jit(solution)/shard_map/dot_general | solution.py:499
  (2 shorter events, 0.0 us)
Async XLA Ops:
  1.4 17.8 %copy-start.4 = (f32[512,128]{1,0:T(8,128)}, f32[512,128]{1,0:T(8,128)S(1)}, u32[]{:S(2)}) copy-start(f32[512,128]{1,0:T(8,128)S(1)} %get-tuple-element.8.cos_ref) | copy-start | bytes 786436
  1.4 17.8 %copy-start.5 = (f32[512,128]{1,0:T(8,128)}, f32[512,128]{1,0:T(8,128)S(1)}, u32[]{:S(2)}) copy-start(f32[512,128]{1,0:T(8,128)S(1)} %get-tuple-element.9.sin_ref) | copy-start | bytes 786436
  1.4 2.4 %copy-start = (bf16[512,4096]{1,0:T(8,128)(2,1)S(1)}, bf16[512,4096]{1,0:T(8,128)(2,1)}, u32[]{:S(2)}) copy-start(bf16[512,4096]{1,0:T(8,128)(2,1)} %x_ref.3) | copy-start | bytes 12582916
  3.8 2.2 %copy-start.1 = (bf16[4096,4,128]{2,1,0:T(4,128)(2,1)S(1)}, bf16[4096,4,128]{2,1,0:T(4,128)(2,1)}, u32[]{:S(2)}) copy-start(bf16[4096,4,128]{2,1,0:T(4,128)(2,1)} %param.7) | copy-start | bytes 12582916
  6.0 2.2 %copy-start.2 = (bf16[4096,4,128]{2,1,0:T(4,128)(2,1)S(1)}, bf16[4096,4,128]{2,1,0:T(4,128)(2,1)}, u32[]{:S(2)}) copy-start(bf16[4096,4,128]{2,1,0:T(4,128)(2,1)} %param.8) | copy-start | bytes 12582916
  19.2 1.0 copy-start.3

commit v3 on v2

--- a/solution.py
+++ b/solution.py
@@ -32,7 +32,12 @@
 def by_head(mix, rows_ref, start, dst_ref, n_heads):
     size = mix.shape[0]
     per = size // n_heads
-    wide = jnp.concatenate([rows_ref[pl.ds(start, size)], rows_ref[pl.ds(pl.multiple_of(start + size, size), size)]], axis=1)
+    if len(rows_ref.shape) == 3:
+        first = pl.multiple_of(start // n_heads, 2 * per)
+        pair = rows_ref[pl.ds(first, 2 * per)].reshape(2 * size, rows_ref.shape[2])
+        wide = jnp.concatenate([pair[:size], pair[size:]], axis=1)
+    else:
+        wide = jnp.concatenate([rows_ref[pl.ds(start, size)], rows_ref[pl.ds(pl.multiple_of(start + size, size), size)]], axis=1)
     head_dim = wide.shape[1] // 2
     out = jnp.dot(mix, wide, preferred_element_type=jnp.float32).astype(jnp.bfloat16)
     at = pl.multiple_of(start // n_heads, 2 * per)
@@ -59,7 +64,7 @@
         by_head(mix[...], wv_ref, start, wv, n_heads)
         return carry
 
-    lax.fori_loop(0, wk_ref.shape[0] // (2 * MIX), arrange, 0, unroll=2)
+    lax.fori_loop(0, wk_ref.shape[0] // (2 * MIX), arrange, 0, unroll=4)
     acc_k[...] += jnp.dot(x_ref[...], wk[...], preferred_element_type=jnp.float32)
     acc_v[...] += jnp.dot(x_ref[...], wv[...], preferred_element_type=jnp.float32)
 
@@ -103,7 +108,7 @@
             pltpu.VMEM((rows, cols), f32),
             pltpu.VMEM((rows, cols), f32),
         ],
-        compiler_params=pltpu.CompilerParams(dimension_semantics=('arbitrary',), vmem_limit_bytes=40 * 1024 * 1024),
+        compiler_params=pltpu.CompilerParams(dimension_semantics=('arbitrary',), vmem_limit_bytes=62 * 1024 * 1024),
         name='project_kv',
     )(hidden, w_k.reshape(model_dim * n_heads, head_dim), w_v.reshape(model_dim * n_heads, head_dim), cos, sin)
 
@@ -128,8 +133,8 @@
         return jnp.where(pair < self.chips, -1, same)
 
 
-def attention_kernel(plan, x_ref, wq_ref, cos_ref, sin_ref, kv_ref, out_ref, qbuf, qstage, kvbuf, acc, m_ref, l_ref,
-                     ostage, orecv, mix, wraw, wsort, accq, loc_sem, w_sem, pair_send, pair_recv, send_sem, recv_sem):
+def attention_kernel(plan, x_hbm, wq_ref, cos_ref, sin_ref, kv_ref, out_ref, qbuf, qstage, kvbuf, acc, m_ref, l_ref,
+                     ostage, orecv, x_ref, mix, wraw, wsort, accq, loc_sem, x_sem, w_sem, pair_send, pair_recv, send_sem, recv_sem):
     me = lax.axis_index('cp')
     chip = me // 2
     core = lax.rem(me, 2)
@@ -162,15 +167,18 @@
     pairs = [plan.pair(chip, s) for s in range(2)]
     own_sub = [core, other]
 
-    n_heads = 2 * heads_j * group
+    n_heads = heads_j * group
     depth = wsort.shape[0]
-    raw_rows = depth * n_heads
-    n_blocks = wq_ref.shape[0] // raw_rows
+    per_half = wq_ref.shape[0] // depth
+    n_blocks = 2 * per_half
+    load_x = pltpu.make_async_copy(x_hbm, x_ref, x_sem)
+    load_x.start()
 
     def fetch(block):
-        at = pl.multiple_of(block * raw_rows, raw_rows)
+        at = pl.multiple_of(lax.rem(block, per_half) * depth, depth)
+        half = jnp.where(block < per_half, other, core)
         slot = lax.rem(block, 2)
-        return pltpu.make_async_copy(wq_ref.at[pl.ds(at, raw_rows)], wraw.at[slot], w_sem.at[slot])
+        return pltpu.make_async_copy(wq_ref.at[pl.ds(at, depth), half], wraw.at[slot], w_sem.at[slot])
 
     fetch(0).start()
 
@@ -243,15 +251,65 @@
         copy.wait_recv()
     for copy in local:
         copy.wait()
-    for s in range(2):
-        send(s, 0, down, always)
-    for step in (1, row - 1):
-        for s in range(2):
-            where = functools.partial(along, s, step)
-            send(s, 0, where, lambda w=where: w() > 0)
+    near, far = 1, row - 1
+
+    def col_of(side):
+        return lax.rem(pairs[side], row)
+
+    def inner(side):
+        return (col_of(side) > 0) & (col_of(side) < row - 1)
+
+    def launch(side, slot, cond):
+        send(side, slot, down, cond)
+        if slot == 0 or slot == row:
+            for step in (1, row - 1):
+                where = functools.partial(along, side, step)
+                send(side, slot, where, lambda w=where: cond() & ((w() > 0) if slot == 0 else (w() < 0)))
+        elif slot == near:
+            send(side, slot, lambda: 1, lambda: cond() & inner(side))
+        elif slot == far:
+            send(side, slot, lambda: -1, lambda: cond() & inner(side))
+
+    def echo(slot):
+        def as_high(d):
+            return plan.twin(pairs[1], d) == slot
+        for d in range(1, row + 1):
+            if (d - slot) % 2 == 1 and d > slot:
+                send(1, d, down, lambda d=d: as_high(d))
+
+    def event(side, slot):
+        arrive(side, slot)
+        if side == 0:
+            launch(0, slot, always)
+            echo(slot)
+        else:
+            launch(1, slot, lambda: plan.twin(pairs[1], slot) < 0)
+
+    launch(0, 0, always)
+    launch(1, 0, always)
+    echo(0)
 
     mix[...] = spread(n_heads, MIX)
-    accq[...] = jnp.zeros_like(accq)
+    load_x.wait()
+
+    def turn(s, half):
+        rows = slice(s * chunk, (s + 1) * chunk)
+        for j in range(heads_j):
+            for g in range(group):
+                col = (j * group + g) * head_dim
+                q = accq[rows, col:col + head_dim].astype(jnp.bfloat16).astype(jnp.float32)
+                q = q * cos_ref[rows] + pltpu.roll(q, head_dim // 2, 1) * sin_ref[rows]
+                q = (q * head_dim ** -0.5).astype(jnp.bfloat16)
+
+                @pl.when(half == 0)
+                def _():
+                    qstage[s, j, g] = q
+
+                @pl.when(half == 1)
+                def _():
+                    qbuf[s, own_sub[s], j, g] = q
+
+    wave = (row, near, far, 2)
 
     def project(block, carry):
         fetch(block).wait()
@@ -260,61 +318,61 @@
         def _():
             fetch(block + 1).start()
 
+        half = block // per_half
+        step = lax.rem(block, per_half)
         raw = wraw.at[lax.rem(block, 2)]
 
         def arrange(i, c):
             by_head(mix[...], raw, pl.multiple_of(i * (2 * MIX), 2 * MIX), wsort, n_heads)
             return c
 
-        lax.fori_loop(0, raw_rows // (2 * MIX), arrange, 0, unroll=4)
-        at = pl.multiple_of(block * depth, depth)
-        accq[...] += jnp.dot(x_ref[:, pl.ds(at, depth)], wsort[...], preferred_element_type=jnp.float32)
+        lax.fori_loop(0, depth * n_heads // (2 * MIX), arrange, 0, unroll=8)
+        at = pl.multiple_of(step * depth, depth)
+        part = jnp.dot(x_ref[:, pl.ds(at, depth)], wsort[...], preferred_element_type=jnp.float32)
+
+        @pl.when(step == 0)
+        def _():
+            accq[...] = part
+
+        @pl.when(step > 0)
+        def _():
+            accq[...] += part
+
+        @pl.when(step == per_half - 1)
+        def _():
+            for s in range(2):
+                turn(s, half)
+
+        @pl.when(block == per_half - 1)
+        def _():
+            for copy in pair_q:
+                copy.start()
+
+        @pl.when(block == n_blocks - 3)
+        def _():
+            event(0, wave[0])
+            event(1, wave[0])
         return carry
 
     lax.fori_loop(0, n_blocks, project, 0)
-
-    def turn(s, half, put):
-        rows = pl.ds(pl.multiple_of(s * chunk, chunk), chunk)
-        for j in range(heads_j):
-            for g in range(group):
-                col = pl.multiple_of(half * half_cols, half_cols) + (j * group + g) * head_dim
-                q = accq[rows, pl.ds(pl.multiple_of(col, head_dim), head_dim)].astype(jnp.bfloat16).astype(jnp.float32)
-                q = q * cos_ref[rows] + pltpu.roll(q, head_dim // 2, 1) * sin_ref[rows]
-                put(j, g, (q * head_dim ** -0.5).astype(jnp.bfloat16))
-
-    def for_partner(s, carry):
-        def put(j, g, q):
-            qstage[s, j, g] = q
-        turn(s, other, put)
-        return carry
-
-    def for_me(s, carry):
-        def put(j, g, q):
-            qbuf[s, jnp.where(s == 0, core, other), j, g] = q
-        turn(s, core, put)
-        return carry
-
-    lax.fori_loop(0, 2, for_partner, 0)
-    lax.fori_loop(0, 2, for_me, 0)
-    for copy in pair_q:
-        copy.start()
     for copy in pair_q:
         copy.wait_recv()
 
-    def block(side, slot_side, slot, j, a, masked, edge):
+    def block(side, slot_side, slot, j, subs, masked, edge):
         k = kvbuf[slot_side, slot, :, 0, j].reshape(2 * chunk, head_dim)
         v = kvbuf[slot_side, slot, :, 1, j].reshape(2 * chunk, head_dim)
-        scores = []
-        for g in range(group):
-            scores.append(lax.dot_general(qbuf[side, a, j, g], k, (((1,), (1,)), ((), ())), preferred_element_type=jnp.float32))
-        if masked:
-            rows = lax.broadcasted_iota(jnp.int32, (chunk, 2 * chunk), 0) + a * chunk
-            cols = lax.broadcasted_iota(jnp.int32, (chunk, 2 * chunk), 1)
-            allowed = (cols > rows) if edge else (cols <= rows)
-        for g in range(group):
-            s = scores[g]
+        tiles = [(a, g) for a in subs for g in range(group)]
+
+        def score(t):
+            a, g = tiles[t]
+            return lax.dot_general(qbuf[side, a, j, g], k, (((1,), (1,)), ((), ())), preferred_element_type=jnp.float32)
+
+        def update(t, s):
+            a, g = tiles[t]
             if masked:
-                s = jnp.where(allowed, s, NEG)
+                rows = lax.broadcasted_iota(jnp.int32, (chunk, 2 * chunk), 0) + a * chunk
+                cols = lax.broadcasted_iota(jnp.int32, (chunk, 2 * chunk), 1)
+                s = jnp.where((cols > rows) if edge else (cols <= rows), s, NEG)
             m_old = m_ref[side, a, j, g]
             m_new = jnp.maximum(m_old, jnp.max(s, axis=1, keepdims=True))
             alpha = jnp.exp(m_old - m_new)
@@ -326,6 +384,13 @@
             l_ref[side, a, j, g] = l_ref[side, a, j, g] * alpha + part
             acc[side, a, j, g] = acc[side, a, j, g] * alpha + jnp.dot(e.astype(jnp.bfloat16), v, preferred_element_type=jnp.float32)
 
+        ahead = 2
+        scores = [score(t) for t in range(ahead)]
+        for t in range(len(tiles)):
+            if t + ahead < len(tiles):
+                scores.append(score(t + ahead))
+            update(t, scores[t])
+
     def sweep(side, slot, masked=False, edge=False):
         slot_side, at = held(side, slot) if isinstance(side, int) else (
             jnp.where(plan.twin(jnp.where(side == 0, pairs[0], pairs[1]), slot) >= 0, 0, side),
@@ -336,67 +401,67 @@
         @pl.when(mine - slot >= 0)
         def _():
             def body(i, carry):
-                block(side, slot_side, at, i // 2, lax.rem(i, 2), masked, edge)
+                block(side, slot_side, at, i, (0, 1), masked, edge)
                 return carry
-            lax.fori_loop(0, heads_j * 2, body, 0)
+            lax.fori_loop(0, heads_j, body, 0)
 
     lax.fori_loop(0, 2, lambda s, c: (sweep(s, 0, True, False), c)[1], 0)
 
-    def hand_on(side, cond):
-        for step in (1, row - 1):
-            where = functools.partial(along, side, step)
-            send(side, row, where, lambda w=where: cond() & (w() < 0))
-        send(side, row, down, cond)
-
-    def single():
-        return plan.twin(pairs[1], row) < 0
-
-    def double():
-        return plan.twin(pairs[1], row) >= 0
-
-    near, far = 1, row - 1
-
-    def pass_on(side, slot):
-        def inner():
-            col = lax.rem(pairs[side], row)
-            return (col > 0) & (col < row - 1)
-
-        send(side, slot, down, always)
-        if slot == near:
-            send(side, slot, lambda: 1, inner)
-        if slot == far:
-            send(side, slot, lambda: -1, inner)
+    def finish(s):
+        def body(i, carry):
+            a = jnp.where(i == 0, 1 - own_sub[s], own_sub[s])
+            for j in range(heads_j):
+                for g in range(group):
+                    total = jnp.sum(l_ref[s, a, j, g], axis=1, keepdims=True)
+                    o = (acc[s, a, j, g] / total).astype(jnp.bfloat16)
+                    col = (j * group + g) * head_dim
+                    ostage[1 - i, s, :, col:col + head_dim] = o
+            return carry
+
+        lax.fori_loop(0, 2, body, 0)
+
+    def back(s):
+        return pltpu.make_async_remote_copy(
+            src_ref=ostage.at[1, s], dst_ref=orecv.at[s], send_sem=pair_send.at[4 + s], recv_sem=pair_recv.at[4 + s],
+            device_id=partner, device_id_type=pl.DeviceIdType.MESH)
+
+    def low_done():
+        finish(0)
+        back(0).start()
+
+    def events(*which):
+        def run():
+            for side, slot in which:
+                event(side, slot)
+        return run
 
     def come(side, slot):
-        def event():
-            arrive(side, slot)
-            if slot < row:
-                pass_on(side, slot)
-        return event
-
-    def first():
-        arrive(0, row)
-        hand_on(0, always)
-        arrive(1, row)
-        hand_on(1, single)
-
+        return lambda: arrive(side, slot)
+
+    def nothing():
+        return None
+
+    w = wave
     order = [
-        (0, 4, first), (0, 1, come(0, 1)), (1, 1, come(1, 1)), (0, 3, come(0, 3)), (0, 2, come(0, 2)), (1, 3, come(1, 3)),
-        (1, 2, come(1, 2)), (1, 4, lambda: hand_on(1, double)),
-        (0, 8, come(0, 8)), (0, 5, come(0, 5)), (1, 5, come(1, 5)), (0, 7, come(0, 7)), (1, 8, come(1, 8)),
-        (0, 6, come(0, 6)), (1, 6, come(1, 6)), (1, 7, come(1, 7)),
+        (0, w[0], events((0, w[1]), (1, w[1]))),
+        (0, w[1], events((0, w[2]), (1, w[2]))),
+        (0, w[2], events((0, w[3]), (1, w[3]))),
+        (0, w[3], nothing),
+        (1, w[0], nothing), (1, w[1], nothing), (1, w[2], nothing), (1, w[3], nothing),
+        (0, 5, come(0, 5)), (0, 7, come(0, 7)), (1, 5, come(1, 5)), (1, 8, come(1, 8)), (0, 8, come(0, 8)),
+        (0, 6, come(0, 6)), (1, 7, lambda: (low_done(), arrive(1, 7))), (1, 6, come(1, 6)),
     ]
 
     def visit(i, carry):
         side = jnp.int32(0)
         slot = jnp.int32(0)
-        for n, (s, d, event) in enumerate(order):
+        for n, (s, d, prepare) in enumerate(order):
             side = jnp.where(i == n, s, side)
             slot = jnp.where(i == n, d, slot)
-
-            @pl.when(i == n)
-            def _():
-                event()
+            if prepare is not nothing:
+                @pl.when(i == n)
+                def _():
+                    prepare()
 
         @pl.when(slot < plan.span)
         def _():
@@ -408,32 +473,17 @@
         return carry
 
     lax.fori_loop(0, len(order), visit, 0)
+    finish(1)
+    back(1).start()
 
     first_col = pl.multiple_of(core * half_cols, half_cols)
-    back_col = pl.multiple_of(core * half_cols, half_cols)
-
-    def finish(i, carry):
-        s = i // 2
-        a = lax.rem(i, 2)
-        mine = a == jnp.where(s == 0, core, other)
-        for j in range(heads_j):
-            for g in range(group):
-                total = jnp.sum(l_ref[s, a, j, g], axis=1, keepdims=True)
-                o = (acc[s, a, j, g] / total).astype(jnp.bfloat16)
-                col = (j * group + g) * head_dim
-                ostage[jnp.where(mine, 0, 1), s, :, col:col + head_dim] = o
-        return carry
-
-    lax.fori_loop(0, 4, finish, 0)
-    back = pltpu.make_async_remote_copy(
-        src_ref=ostage.at[1], dst_ref=orecv, send_sem=pair_send.at[4], recv_sem=pair_recv.at[4],
-        device_id=partner, device_id_type=pl.DeviceIdType.MESH)
-    back.start()
     other_col = pl.multiple_of(other * half_cols, half_cols)
     out_ref[:, :, pl.ds(first_col, half_cols)] = ostage[0]
-    back.wait_recv()
-    out_ref[:, :, pl.ds(other_col, half_cols)] = orecv[...]
-    back.wait_send()
+    for s in range(2):
+        back(s).wait_recv()
+        out_ref[s, :, pl.ds(other_col, half_cols)] = orecv[s]
+    for s in range(2):
+        back(s).wait_send()
     for copy in pair_kv + pair_q:
         copy.wait_send()
     for spec in sent:
@@ -450,12 +500,14 @@
     group = heads // (2 * heads_j)
     bf16, f32 = jnp.bfloat16, jnp.float32
     slots = plan.span + 1
-    depth = model_dim // 8
+    half_heads = heads // 2
+    depth = model_dim // 4
     vmem = pl.BlockSpec(memory_space=pltpu.VMEM)
+    anywhere = pl.BlockSpec(memory_space=pl.ANY)
     return pl.pallas_call(
         functools.partial(attention_kernel, plan),
         out_shape=jax.ShapeDtypeStruct((2, chunk, heads * head_dim), bf16),
-        in_specs=[vmem, pl.BlockSpec(memory_space=pl.ANY), vmem, vmem, vmem],
+        in_specs=[anywhere, anywhere, vmem, vmem, vmem],
         out_specs=vmem,
         scratch_shapes=[
             pltpu.VMEM((2, 2, heads_j, group, chunk, head_dim), bf16),
@@ -466,20 +518,22 @@
             pltpu.VMEM((2, 2, heads_j, group, chunk, head_dim), f32),
             pltpu.VMEM((2, 2, chunk, heads_j * group * head_dim), bf16),
             pltpu.VMEM((2, chunk, heads_j * group * head_dim), bf16),
+            pltpu.VMEM((2 * chunk, model_dim), bf16),
             pltpu.VMEM((MIX, MIX), bf16),
-            pltpu.VMEM((2, depth * heads, head_dim), bf16),
-            pltpu.VMEM((depth, heads * head_dim), bf16),
-            pltpu.VMEM((2 * chunk, heads * head_dim), f32),
+            pltpu.VMEM((2, depth, half_heads, head_dim), bf16),
+            pltpu.VMEM((depth, half_heads * head_dim), bf16),
+            pltpu.VMEM((2 * chunk, half_heads * head_dim), f32),
             pltpu.SemaphoreType.DMA((2,)),
+            pltpu.SemaphoreType.DMA,
             pltpu.SemaphoreType.DMA((2,)),
-            pltpu.SemaphoreType.DMA((5,)),
-            pltpu.SemaphoreType.DMA((5,)),
+            pltpu.SemaphoreType.DMA((6,)),
+            pltpu.SemaphoreType.DMA((6,)),
             pltpu.SemaphoreType.DMA((64,)),
             pltpu.SemaphoreType.DMA((2, slots)),
         ],
-        compiler_params=pltpu.CompilerParams(collective_id=0, has_side_effects=True, vmem_limit_bytes=60 * 1024 * 1024),
+        compiler_params=pltpu.CompilerParams(collective_id=0, has_side_effects=True, vmem_limit_bytes=62 * 1024 * 1024),
         name='attend',
-    )(hidden, w_q.reshape(model_dim * heads, head_dim), cos, sin, kv_all)
+    )(hidden, w_q.reshape(model_dim, 2, half_heads, head_dim), cos, sin, kv_all)
 
 
 def solution(mesh):

time: 170 us -> 142 us (0.84)
  the two profiles are of different devices: /device:TPU:117 before, /device:TPU:123 now
where the time goes in v3:
time: 142 us
  Pallas kernels  126 us (89%)
  matrix products  14.3 us (10%)
  other arithmetic  2.15 us (2%)
    pallas_call x1, Pallas kernels, attend(): pl.pallas_call(functools.partial(attention_kernel, plan), out_shape=jax.S...  113 us
    dot_general x1, matrix products, device_step(): jnp.dot(attended.reshape(2 * chunk_len, heads * head_dim), w_o.reshape(he...  14.3 us
    pallas_call x1, Pallas kernels, project_kv(): pl.pallas_call(functools.partial(kv_kernel, n_heads), grid=(model_dim //...  13 us

profile of v3, /device:TPU:123, one launch (start us, length us, event | category | flops | bytes accessed | tf_op | source)
XLA Modules:
  0.0 142.3 jit_solution(16088402556770170076)
XLA Ops:
  0.0 0.1 add_multiply_fusion
  0.1 0.1 convert_bitcast_fusion
  0.2 1.0 fusion
  1.2 1.0 pad_maximum_fusion
  2.2 13.0 %project_kv.1.kv_ref = bf16[2,2,2,2,256,128]{5,4,3,2,1,0:T(8,128)(2,1)} custom-call(bf16[512,4096]{1,0:T(8,128)(2,1)} %x_hbm.1, bf16[16384,128]{1,0:T(8,128)(2,1)} %bitcast.13, bf16[16384,128]{1,0:T(8,128)(2,1)} %bitcast.14, f32[512,128]{1,0:T(8,128)} %get-tuple-element.8.cos_ref, f32[512,128]{1,0:T(8,128)} %get-tuple-element.9.sin_ref), custom_call_target="tpu_custom_call" | custom-call | tf_op jit(solution)/shard_map/project_kv/pallas_call | solution.py:92
  15.2 112.8 %attend.1 = bf16[2,256,2048]{2,1,0:T(8,128)(2,1)} custom-call(bf16[512,4096]{1,0:T(8,128)(2,1)} %x_hbm.1, bf16[4096,2,8,128]{3,2,1,0:T(8,128)(2,1)} %bitcast.12, f32[512,128]{1,0:T(8,128)} %get-tuple-element.8.cos_ref, f32[512,128]{1,0:T(8,128)} %get-tuple-element.9.sin_ref, bf16[2,2,2,2,256,128]{5,4,3,2,1,0:T(8,128)(2,1)} %project_kv.1.kv_ref), custom_call_target="tpu_custom_call" | custom-call | tf_op jit(solution)/shard_map/attend/pallas_call | solution.py:507
  128.0 14.3 %convolution_convert_fusion = bf16[512,4096]{1,0:T(8,128)(2,1)} fusion(bf16[512,2048]{1,0:T(8,128)(2,1)} %bitcast.15, bf16[2048,4096]{1,0:T(8,128)(2,1)} %bitcast.17), kind=kOutput, calls=%fused_computation | convolution fusion | flops 8592031744 | bytes 23068672 | tf_op jit(solution)/shard_map/dot_general | solution.py:553
  (2 shorter events, 0.0 us)

commit v4 on v3

--- a/solution.py
+++ b/solution.py
@@ -29,7 +29,7 @@
     return jnp.where((to % per) * n_heads + to // per == of, 1.0, 0.0).astype(jnp.bfloat16)
 
 
-def by_head(mix, rows_ref, start, dst_ref, n_heads):
+def by_head(mix, rows_ref, start, dst_ref, n_heads, base=0):
     size = mix.shape[0]
     per = size // n_heads
     if len(rows_ref.shape) == 3:
@@ -40,7 +40,7 @@
         wide = jnp.concatenate([rows_ref[pl.ds(start, size)], rows_ref[pl.ds(pl.multiple_of(start + size, size), size)]], axis=1)
     head_dim = wide.shape[1] // 2
     out = jnp.dot(mix, wide, preferred_element_type=jnp.float32).astype(jnp.bfloat16)
-    at = pl.multiple_of(start // n_heads, 2 * per)
+    at = base + pl.multiple_of(start // n_heads, 2 * per)
     for b in range(2):
         for h in range(n_heads):
             dst_ref[pl.ds(pl.multiple_of(at + b * per, per), per), h * head_dim:(h + 1) * head_dim] = out[h * per:(h + 1) * per, b * head_dim:(b + 1) * head_dim]
@@ -133,8 +133,8 @@
         return jnp.where(pair < self.chips, -1, same)
 
 
-def attention_kernel(plan, x_hbm, wq_ref, cos_ref, sin_ref, kv_ref, out_ref, qbuf, qstage, kvbuf, acc, m_ref, l_ref,
-                     ostage, orecv, x_ref, mix, wraw, wsort, accq, loc_sem, x_sem, w_sem, pair_send, pair_recv, send_sem, recv_sem):
+def attention_kernel(plan, x_hbm, wq_ref, cos_in, sin_in, kv_ref, out_ref, qbuf, kvbuf, acc, m_ref, l_ref,
+                     ostage, orecv, x_ref, turns, mix, wraw, wsort, loc_sem, x_sem, w_sem, pair_send, pair_recv, send_sem, recv_sem):
     me = lax.axis_index('cp')
     chip = me // 2
     core = lax.rem(me, 2)
@@ -168,33 +168,39 @@
     own_sub = [core, other]
 
     n_heads = heads_j * group
-    depth = wsort.shape[0]
-    per_half = wq_ref.shape[0] // depth
-    n_blocks = 2 * per_half
-    load_x = pltpu.make_async_copy(x_hbm, x_ref, x_sem)
-    load_x.start()
+    depth = wraw.shape[1]
+    n_blocks = wq_ref.shape[0] // depth
+    load_x = pltpu.make_async_copy(x_hbm, x_ref.at[0], x_sem)
 
     def fetch(block):
-        at = pl.multiple_of(lax.rem(block, per_half) * depth, depth)
-        half = jnp.where(block < per_half, other, core)
+        at = pl.multiple_of(block * depth, depth)
         slot = lax.rem(block, 2)
-        return pltpu.make_async_copy(wq_ref.at[pl.ds(at, depth), half], wraw.at[slot], w_sem.at[slot])
+        return pltpu.make_async_copy(wq_ref.at[pl.ds(at, depth), core], wraw.at[slot], w_sem.at[slot])
 
     fetch(0).start()
 
     pair_kv = []
-    pair_q = []
     local = []
     for s in range(2):
         pair_kv.append(pltpu.make_async_remote_copy(
             src_ref=kv_ref.at[other, s], dst_ref=kvbuf.at[s, 0, own_sub[s]], send_sem=pair_send.at[s],
             recv_sem=pair_recv.at[s], device_id=partner, device_id_type=pl.DeviceIdType.MESH))
-        pair_q.append(pltpu.make_async_remote_copy(
-            src_ref=qstage.at[s], dst_ref=qbuf.at[s, own_sub[s]], send_sem=pair_send.at[2 + s],
-            recv_sem=pair_recv.at[2 + s], device_id=partner, device_id_type=pl.DeviceIdType.MESH))
         local.append(pltpu.make_async_copy(kv_ref.at[core, s], kvbuf.at[s, 0, own_sub[s]], loc_sem.at[s]))
     for copy in pair_kv + local:
         copy.start()
+    pair_x = pltpu.make_async_remote_copy(
+        src_ref=x_hbm, dst_ref=x_ref.at[1], send_sem=pair_send.at[2], recv_sem=pair_recv.at[2],
+        device_id=partner, device_id_type=pl.DeviceIdType.MESH)
+    pair_x.start()
+    load_x.start()
+    pair_turn = []
+    for t, table in enumerate((cos_in, sin_in)):
+        local.append(pltpu.make_async_copy(table, turns.at[0, t], loc_sem.at[2 + t]))
+        local[-1].start()
+        pair_turn.append(pltpu.make_async_remote_copy(
+            src_ref=table, dst_ref=turns.at[1, t], send_sem=pair_send.at[6 + t], recv_sem=pair_recv.at[6 + t],
+            device_id=partner, device_id_type=pl.DeviceIdType.MESH))
+        pair_turn[-1].start()
 
     acc[...] = jnp.zeros_like(acc)
     l_ref[...] = jnp.zeros_like(l_ref)
@@ -270,93 +276,76 @@
         elif slot == far:
             send(side, slot, lambda: -1, lambda: cond() & inner(side))
 
-    def echo(slot):
+    def echo(slot, cond=lambda: pairs[0] >= 0):
         def as_high(d):
             return plan.twin(pairs[1], d) == slot
         for d in range(1, row + 1):
             if (d - slot) % 2 == 1 and d > slot:
-                send(1, d, down, lambda d=d: as_high(d))
-
-    def event(side, slot):
-        arrive(side, slot)
+                send(1, d, down, lambda d=d: as_high(d) & cond())
+
+    def event(side, slot, cond=always):
+        arrive(side, slot, cond())
         if side == 0:
-            launch(0, slot, always)
-            echo(slot)
+            launch(0, slot, cond)
+            echo(slot, cond)
         else:
-            launch(1, slot, lambda: plan.twin(pairs[1], slot) < 0)
+            launch(1, slot, lambda: cond() & (plan.twin(pairs[1], slot) < 0))
 
     launch(0, 0, always)
     launch(1, 0, always)
     echo(0)
 
     mix[...] = spread(n_heads, MIX)
+
+    def sort(block, carry):
+        fetch(block).wait()
+
+        @pl.when(block + 1 < n_blocks)
+        def _():
+            fetch(block + 1).start()
+
+        raw = wraw.at[lax.rem(block, 2)]
+        base = pl.multiple_of(block * depth, depth)
+
+        def arrange(i, c):
+            by_head(mix[...], raw, pl.multiple_of(i * (2 * MIX), 2 * MIX), wsort, n_heads, base)
+            return c
+
+        lax.fori_loop(0, depth * n_heads // (2 * MIX), arrange, 0, unroll=8)
+        return carry
+
+    lax.fori_loop(0, n_blocks, sort, 0)
     load_x.wait()
-
-    def turn(s, half):
-        rows = slice(s * chunk, (s + 1) * chunk)
-        for j in range(heads_j):
-            for g in range(group):
-                col = (j * group + g) * head_dim
-                q = accq[rows, col:col + head_dim].astype(jnp.bfloat16).astype(jnp.float32)
-                q = q * cos_ref[rows] + pltpu.roll(q, head_dim // 2, 1) * sin_ref[rows]
-                q = (q * head_dim ** -0.5).astype(jnp.bfloat16)
-
-                @pl.when(half == 0)
-                def _():
-                    qstage[s, j, g] = q
-
-                @pl.when(half == 1)
-                def _():
-                    qbuf[s, own_sub[s], j, g] = q
-
-    wave = (row, near, far, 2)
-
-    def project(block, carry):
-        fetch(block).wait()
-
-        @pl.when(block + 1 < n_blocks)
-        def _():
-            fetch(block + 1).start()
-
-        half = block // per_half
-        step = lax.rem(block, per_half)
-        raw = wraw.at[lax.rem(block, 2)]
-
-        def arrange(i, c):
-            by_head(mix[...], raw, pl.multiple_of(i * (2 * MIX), 2 * MIX), wsort, n_heads)
-            return c
-
-        lax.fori_loop(0, depth * n_heads // (2 * MIX), arrange, 0, unroll=8)
-        at = pl.multiple_of(step * depth, depth)
-        part = jnp.dot(x_ref[:, pl.ds(at, depth)], wsort[...], preferred_element_type=jnp.float32)
-
-        @pl.when(step == 0)
-        def _():
-            accq[...] = part
-
-        @pl.when(step > 0)
-        def _():
-            accq[...] += part
-
-        @pl.when(step == per_half - 1)
-        def _():
-            for s in range(2):
-                turn(s, half)
-
-        @pl.when(block == per_half - 1)
-        def _():
-            for copy in pair_q:
-                copy.start()
-
-        @pl.when(block == n_blocks - 3)
-        def _():
-            event(0, wave[0])
-            event(1, wave[0])
+    wide = 2
+    per_rows = n_heads // wide
+
+    def project(i, carry):
+        whose = i // per_rows
+        first = lax.rem(i, per_rows) * wide
+
+        @pl.when(i == per_rows)
+        def _():
+            pair_x.wait_recv()
+            for copy in pair_turn:
+                copy.wait_recv()
+
+        cols = pl.ds(pl.multiple_of(first * head_dim, wide * head_dim), wide * head_dim)
+        part = jnp.dot(x_ref[whose], wsort[:, cols], preferred_element_type=jnp.float32)
+        for s in range(2):
+            rows = slice(s * chunk, (s + 1) * chunk)
+            sub = jnp.where(whose == 0, own_sub[s], 1 - own_sub[s])
+            for h in range(wide):
+                q = part[rows, h * head_dim:(h + 1) * head_dim].astype(jnp.bfloat16).astype(jnp.float32)
+                q = q * turns[whose, 0, rows] + pltpu.roll(q, head_dim // 2, 1) * turns[whose, 1, rows]
+                qbuf[s, sub, first // group, lax.rem(first, group) + h] = (q * head_dim ** -0.5).astype(jnp.bfloat16)
+
+        @pl.when(i == 2 * per_rows - 2)
+        def _():
+            event(0, row)
+            event(1, row)
         return carry
 
-    lax.fori_loop(0, n_blocks, project, 0)
-    for copy in pair_q:
-        copy.wait_recv()
+    lax.fori_loop(0, 2 * per_rows, project, 0)
 
     def block(side, slot_side, slot, j, subs, masked, edge):
         k = kvbuf[slot_side, slot, :, 0, j].reshape(2 * chunk, head_dim)
@@ -405,6 +394,8 @@
                 return carry
             lax.fori_loop(0, heads_j, body, 0)
 
+    for s in range(2):
+        event(s, near, lambda s=s: col_of(s) > 0)
     lax.fori_loop(0, 2, lambda s, c: (sweep(s, 0, True, False), c)[1], 0)
 
     def finish(s):
@@ -429,45 +420,51 @@
         finish(0)
         back(0).start()
 
-    def events(*which):
+    def come(*which):
         def run():
             for side, slot in which:
-                event(side, slot)
+                arrive(side, slot)
         return run
 
-    def come(side, slot):
-        return lambda: arrive(side, slot)
+    def far_events():
+        for s in range(2):
+            event(s, far)
+        for s in range(2):
+            event(s, near, lambda s=s: col_of(s) == 0)
 
     def nothing():
         return None
 
-    w = wave
     order = [
-        (0, w[0], events((0, w[1]), (1, w[1]))),
-        (0, w[1], events((0, w[2]), (1, w[2]))),
-        (0, w[2], events((0, w[3]), (1, w[3]))),
-        (0, w[3], nothing),
-        (1, w[0], nothing), (1, w[1], nothing), (1, w[2], nothing), (1, w[3], nothing),
-        (0, 5, come(0, 5)), (0, 7, come(0, 7)), (1, 5, come(1, 5)), (1, 8, come(1, 8)), (0, 8, come(0, 8)),
-        (0, 6, come(0, 6)), (1, 7, lambda: (low_done(), arrive(1, 7))), (1, 6, come(1, 6)),
+        (0, row, 0, nothing), (1, row, 1, nothing),
+        (0, near, 0, far_events), (1, near, 0, nothing), (0, far, 0, nothing), (1, far, 1, nothing),
+        (1, 2, 0, lambda: event(1, 2)), (0, 8, 0, come((0, 8))), (0, 2, 0, lambda: event(0, 2)),
+        (1, row, 2, nothing), (1, far, 2, nothing),
+        (0, 5, 0, come((0, 5))), (1, 5, 0, come((1, 5))), (0, 7, 0, come((0, 7))), (1, 8, 0, come((1, 8))),
+        (0, 6, 0, come((0, 6))), (1, 7, 0, lambda: (low_done(), arrive(1, 7))), (1, 6, 0, come((1, 6))),
     ]
 
     def visit(i, carry):
         side = jnp.int32(0)
         slot = jnp.int32(0)
-        for n, (s, d, prepare) in enumerate(order):
+        kind = jnp.int32(0)
+        for n, (s, d, when, prepare) in enumerate(order):
             side = jnp.where(i == n, s, side)
             slot = jnp.where(i == n, d, slot)
+            kind = jnp.where(i == n, when, kind)
             if prepare is not nothing:
                 @pl.when(i == n)
                 def _():
                     prepare()
 
-        @pl.when(slot < plan.span)
+        doubled = plan.twin(jnp.where(side == 0, pairs[0], pairs[1]), slot) >= 0
+        due = (kind == 0) | ((kind == 1) & jnp.logical_not(doubled)) | ((kind == 2) & doubled)
+
+        @pl.when(due & (slot < plan.span))
         def _():
             sweep(side, slot)
 
-        @pl.when(slot == plan.span)
+        @pl.when(due & (slot == plan.span))
         def _():
             sweep(side, slot, True, True)
         return carry
@@ -484,7 +481,7 @@
         out_ref[s, :, pl.ds(other_col, half_cols)] = orecv[s]
     for s in range(2):
         back(s).wait_send()
-    for copy in pair_kv + pair_q:
+    for copy in pair_kv + [pair_x] + pair_turn:
         copy.wait_send()
     for spec in sent:
         copy, ok = describe(*spec)
@@ -511,23 +508,22 @@
         out_specs=vmem,
         scratch_shapes=[
             pltpu.VMEM((2, 2, heads_j, group, chunk, head_dim), bf16),
-            pltpu.VMEM((2, heads_j, group, chunk, head_dim), bf16),
             pltpu.VMEM((2, slots, 2, 2, heads_j, chunk, head_dim), bf16),
             pltpu.VMEM((2, 2, heads_j, group, chunk, head_dim), f32),
             pltpu.VMEM((2, 2, heads_j, group, chunk, head_dim), f32),
             pltpu.VMEM((2, 2, heads_j, group, chunk, head_dim), f32),
             pltpu.VMEM((2, 2, chunk, heads_j * group * head_dim), bf16),
             pltpu.VMEM((2, chunk, heads_j * group * head_dim), bf16),
-            pltpu.VMEM((2 * chunk, model_dim), bf16),
+            pltpu.VMEM((2, 2 * chunk, model_dim), bf16),
+            pltpu.VMEM((2, 2, 2 * chunk, head_dim), f32),
             pltpu.VMEM((MIX, MIX), bf16),
             pltpu.VMEM((2, depth, half_heads, head_dim), bf16),
-            pltpu.VMEM((depth, half_heads * head_dim), bf16),
-            pltpu.VMEM((2 * chunk, half_heads * head_dim), f32),
-            pltpu.SemaphoreType.DMA((2,)),
+            pltpu.VMEM((model_dim, half_heads * head_dim), bf16),
+            pltpu.SemaphoreType.DMA((4,)),
             pltpu.SemaphoreType.DMA,
             pltpu.SemaphoreType.DMA((2,)),
-            pltpu.SemaphoreType.DMA((6,)),
-            pltpu.SemaphoreType.DMA((6,)),
+            pltpu.SemaphoreType.DMA((8,)),
+            pltpu.SemaphoreType.DMA((8,)),
             pltpu.SemaphoreType.DMA((64,)),
             pltpu.SemaphoreType.DMA((2, slots)),
         ],

time: 142 us -> 128 us (0.901)
  the two profiles are of different devices: /device:TPU:123 before, /device:TPU:125 now
where the time goes in v4:
time: 128 us
  Pallas kernels  111 us (87%)
  matrix products  14.3 us (11%)
  other arithmetic  2.15 us (2%)
    pallas_call x1, Pallas kernels, attend(): pl.pallas_call(functools.partial(attention_kernel, plan), out_shape=jax.S...  98.4 us
    dot_general x1, matrix products, device_step(): jnp.dot(attended.reshape(2 * chunk_len, heads * head_dim), w_o.reshape(he...  14.3 us
    pallas_call x1, Pallas kernels, project_kv(): pl.pallas_call(functools.partial(kv_kernel, n_heads), grid=(model_dim //...  13 us

profile of v4, /device:TPU:125, one launch (start us, length us, event | category | flops | bytes accessed | tf_op | source)
XLA Modules:
  0.0 127.9 jit_solution(2181352009509238220)
XLA Ops:
  0.0 0.1 add_multiply_fusion
  0.1 0.1 convert_bitcast_fusion
  0.2 1.0 fusion
  1.2 1.0 pad_maximum_fusion
  2.2 13.0 %project_kv.1.kv_ref = bf16[2,2,2,2,256,128]{5,4,3,2,1,0:T(8,128)(2,1)} custom-call(bf16[512,4096]{1,0:T(8,128)(2,1)} %x_hbm.1, bf16[16384,128]{1,0:T(8,128)(2,1)} %bitcast.13, bf16[16384,128]{1,0:T(8,128)(2,1)} %bitcast.14, f32[512,128]{1,0:T(8,128)} %get-tuple-element.8.cos_ref.cos_in, f32[512,128]{1,0:T(8,128)} %get-tuple-element.9.sin_ref.sin_in), custom_call_target="tpu_custom_call" | custom-call | tf_op jit(solution)/shard_map/project_kv/pallas_call | solution.py:92
  15.2 98.4 %attend.1 = bf16[2,256,2048]{2,1,0:T(8,128)(2,1)} custom-call(bf16[512,4096]{1,0:T(8,128)(2,1)} %x_hbm.1, bf16[4096,2,8,128]{3,2,1,0:T(8,128)(2,1)} %bitcast.12, f32[512,128]{1,0:T(8,128)} %get-tuple-element.8.cos_ref.cos_in, f32[512,128]{1,0:T(8,128)} %get-tuple-element.9.sin_ref.sin_in, bf16[2,2,2,2,256,128]{5,4,3,2,1,0:T(8,128)(2,1)} %project_kv.1.kv_ref), custom_call_target="tpu_custom_call" | custom-call | tf_op jit(solution)/shard_map/attend/pallas_call | solution.py:504
  113.6 14.3 %convolution_convert_fusion = bf16[512,4096]{1,0:T(8,128)(2,1)} fusion(bf16[512,2048]{1,0:T(8,128)(2,1)} %bitcast.15, bf16[2048,4096]{1,0:T(8,128)(2,1)} %bitcast.17), kind=kOutput, calls=%fused_computation | convolution fusion | flops 8592031744 | bytes 23068672 | tf_op jit(solution)/shard_map/dot_general | solution.py:549
  (2 shorter events, 0.0 us)

commit v5 on v4

--- a/solution.py
+++ b/solution.py
@@ -29,88 +29,22 @@
     return jnp.where((to % per) * n_heads + to // per == of, 1.0, 0.0).astype(jnp.bfloat16)
 
 
-def by_head(mix, rows_ref, start, dst_ref, n_heads, base=0):
+def by_head(mix, rows_ref, start, dst_ref, n_heads, base, col):
     size = mix.shape[0]
     per = size // n_heads
-    if len(rows_ref.shape) == 3:
-        first = pl.multiple_of(start // n_heads, 2 * per)
-        pair = rows_ref[pl.ds(first, 2 * per)].reshape(2 * size, rows_ref.shape[2])
-        wide = jnp.concatenate([pair[:size], pair[size:]], axis=1)
-    else:
-        wide = jnp.concatenate([rows_ref[pl.ds(start, size)], rows_ref[pl.ds(pl.multiple_of(start + size, size), size)]], axis=1)
-    head_dim = wide.shape[1] // 2
+    head_dim = rows_ref.shape[2]
+    first = pl.multiple_of(start // rows_ref.shape[1], 2 * size // rows_ref.shape[1])
+    pair = rows_ref[pl.ds(first, 2 * size // rows_ref.shape[1])].reshape(2 * size, head_dim)
+    wide = jnp.concatenate([pair[:size], pair[size:]], axis=1)
     out = jnp.dot(mix, wide, preferred_element_type=jnp.float32).astype(jnp.bfloat16)
     at = base + pl.multiple_of(start // n_heads, 2 * per)
     for b in range(2):
         for h in range(n_heads):
-            dst_ref[pl.ds(pl.multiple_of(at + b * per, per), per), h * head_dim:(h + 1) * head_dim] = out[h * per:(h + 1) * per, b * head_dim:(b + 1) * head_dim]
+            cols = pl.ds(pl.multiple_of(col + h * head_dim, head_dim), head_dim)
+            dst_ref[pl.ds(pl.multiple_of(at + b * per, per), per), cols] = out[h * per:(h + 1) * per, b * head_dim:(b + 1) * head_dim]
 
 
 MIX = 256
-
-
-def kv_kernel(n_heads, x_ref, wk_ref, wv_ref, cos_ref, sin_ref, out_ref, mix, wk, wv, acc_k, acc_v):
-    step = pl.program_id(0)
-
-    @pl.when(step == 0)
-    def _():
-        mix[...] = spread(n_heads, MIX)
-        acc_k[...] = jnp.zeros_like(acc_k)
-        acc_v[...] = jnp.zeros_like(acc_v)
-
-    def arrange(i, carry):
-        start = pl.multiple_of(i * (2 * MIX), 2 * MIX)
-        by_head(mix[...], wk_ref, start, wk, n_heads)
-        by_head(mix[...], wv_ref, start, wv, n_heads)
-        return carry
-
-    lax.fori_loop(0, wk_ref.shape[0] // (2 * MIX), arrange, 0, unroll=4)
-    acc_k[...] += jnp.dot(x_ref[...], wk[...], preferred_element_type=jnp.float32)
-    acc_v[...] += jnp.dot(x_ref[...], wv[...], preferred_element_type=jnp.float32)
-
-    @pl.when(step == pl.num_programs(0) - 1)
-    def _():
-        chunk, head_dim = out_ref.shape[4], out_ref.shape[5]
-        half = n_heads // 2
-        for n in range(2):
-            rows = slice(n * chunk, (n + 1) * chunk)
-            for h in range(n_heads):
-                cols = slice(h * head_dim, (h + 1) * head_dim)
-                k = acc_k[rows, cols].astype(jnp.bfloat16).astype(jnp.float32)
-                k = k * cos_ref[rows] + pltpu.roll(k, head_dim // 2, 1) * sin_ref[rows]
-                out_ref[h // half, n, 0, h % half] = k.astype(jnp.bfloat16)
-                out_ref[h // half, n, 1, h % half] = acc_v[rows, cols].astype(jnp.bfloat16)
-
-
-def project_kv(hidden, w_k, w_v, cos, sin):
-    rows, model_dim = hidden.shape
-    n_heads, head_dim = w_k.shape[1:]
-    chunk = rows // 2
-    depth = model_dim // 4
-    bf16, f32 = jnp.bfloat16, jnp.float32
-    cols = n_heads * head_dim
-    return pl.pallas_call(
-        functools.partial(kv_kernel, n_heads),
-        grid=(model_dim // depth,),
-        in_specs=[
-            pl.BlockSpec((rows, depth), lambda i: (0, i)),
-            pl.BlockSpec((depth * n_heads, head_dim), lambda i: (i, 0)),
-            pl.BlockSpec((depth * n_heads, head_dim), lambda i: (i, 0)),
-            pl.BlockSpec((rows, head_dim), lambda i: (0, 0)),
-            pl.BlockSpec((rows, head_dim), lambda i: (0, 0)),
-        ],
-        out_specs=pl.BlockSpec((2, 2, 2, n_heads // 2, chunk, head_dim), lambda i: (0, 0, 0, 0, 0, 0)),
-        out_shape=jax.ShapeDtypeStruct((2, 2, 2, n_heads // 2, chunk, head_dim), bf16),
-        scratch_shapes=[
-            pltpu.VMEM((MIX, MIX), bf16),
-            pltpu.VMEM((depth, cols), bf16),
-            pltpu.VMEM((depth, cols), bf16),
-            pltpu.VMEM((rows, cols), f32),
-            pltpu.VMEM((rows, cols), f32),
-        ],
-        compiler_params=pltpu.CompilerParams(dimension_semantics=('arbitrary',), vmem_limit_bytes=62 * 1024 * 1024),
-        name='project_kv',
-    )(hidden, w_k.reshape(model_dim * n_heads, head_dim), w_v.reshape(model_dim * n_heads, head_dim), cos, sin)
 
 
 class Plan:
@@ -133,7 +67,7 @@
         return jnp.where(pair < self.chips, -1, same)
 
 
-def attention_kernel(plan, x_hbm, wq_ref, cos_in, sin_in, kv_ref, out_ref, qbuf, kvbuf, acc, m_ref, l_ref,
+def attention_kernel(plan, kv_heads, x_hbm, wk_ref, wv_ref, wq_ref, cos_in, sin_in, out_ref, kv_ref, qbuf, kvbuf, acc, m_ref, l_ref,
                      ostage, orecv, x_ref, turns, mix, wraw, wsort, loc_sem, x_sem, w_sem, pair_send, pair_recv, send_sem, recv_sem):
     me = lax.axis_index('cp')
     chip = me // 2
@@ -161,7 +95,6 @@
         @pl.when((y + dy >= 0) & (y + dy < n_row))
         def _():
             pl.semaphore_signal(barrier, inc=1, device_id=device(chip + dy * row, core), device_id_type=pl.DeviceIdType.MESH)
-    pl.semaphore_wait(barrier, row + jnp.where(y > 0, 1, 0) + jnp.where(y < n_row - 1, 1, 0))
 
     partner = device(chip, other)
     pairs = [plan.pair(chip, s) for s in range(2)]
@@ -169,15 +102,75 @@
 
     n_heads = heads_j * group
     depth = wraw.shape[1]
-    n_blocks = wq_ref.shape[0] // depth
+    n_kv = wk_ref.shape[0] // depth
+    n_q = wq_ref.shape[0] // depth
     load_x = pltpu.make_async_copy(x_hbm, x_ref.at[0], x_sem)
 
-    def fetch(block):
-        at = pl.multiple_of(block * depth, depth)
+    def fetch(block, part):
+        at = pl.ds(pl.multiple_of(block * depth, depth), depth)
         slot = lax.rem(block, 2)
-        return pltpu.make_async_copy(wq_ref.at[pl.ds(at, depth), core], wraw.at[slot], w_sem.at[slot])
-
-    fetch(0).start()
+        src = (wk_ref.at[at], wv_ref.at[at], wq_ref.at[at, core] if part == 2 else None)[part]
+        return pltpu.make_async_copy(src, wraw.at[slot], w_sem.at[slot])
+
+    fetch(0, 0).start()
+    load_x.start()
+
+    acc[...] = jnp.zeros_like(acc)
+    l_ref[...] = jnp.zeros_like(l_ref)
+    m_ref[...] = jnp.full_like(m_ref, NEG)
+
+    mix[...] = spread(kv_heads, MIX)
+    width = kv_heads * head_dim
+
+    def sort(part, blocks, heads, follow):
+        def step(block, carry):
+            fetch(block, part).wait()
+
+            @pl.when(block + 1 < blocks)
+            def _():
+                fetch(block + 1, part).start()
+
+            @pl.when(block + 1 == blocks)
+            def _():
+                follow()
+
+            raw = wraw.at[lax.rem(block, 2)]
+            rows = depth * raw.shape[1] // heads
+            base = pl.multiple_of(block * rows, rows)
+
+            def arrange(i, c):
+                by_head(mix[...], raw, pl.multiple_of(i * (2 * MIX), 2 * MIX), wsort, heads, base, width if part == 1 else 0)
+                return c
+
+            lax.fori_loop(0, depth * raw.shape[1] // (2 * MIX), arrange, 0, unroll=8)
+            return carry
+
+        lax.fori_loop(0, blocks, step, 0)
+
+    sort(0, n_kv, kv_heads, lambda: fetch(0, 1).start())
+    pl.semaphore_wait(barrier, row + jnp.where(y > 0, 1, 0) + jnp.where(y < n_row - 1, 1, 0))
+    pair_x = pltpu.make_async_remote_copy(
+        src_ref=x_hbm, dst_ref=x_ref.at[1], send_sem=pair_send.at[2], recv_sem=pair_recv.at[2],
+        device_id=partner, device_id_type=pl.DeviceIdType.MESH)
+    pair_x.start()
+    sort(1, n_kv, kv_heads, lambda: fetch(0, 2).start())
+    load_x.wait()
+    wide = 2
+
+    def project_kv(i, carry):
+        first = lax.rem(i, kv_heads // wide)
+        is_key = i < kv_heads // wide
+        cols = pl.ds(pl.multiple_of(i * wide * head_dim, wide * head_dim), wide * head_dim)
+        part = jnp.dot(x_ref[0], wsort[:, cols], preferred_element_type=jnp.float32)
+        for s in range(2):
+            rows = slice(s * chunk, (s + 1) * chunk)
+            for h in range(wide):
+                plain = part[rows, h * head_dim:(h + 1) * head_dim].astype(jnp.bfloat16).astype(jnp.float32)
+                turned = plain * cos_in[rows] + pltpu.roll(plain, head_dim // 2, 1) * sin_in[rows]
+                kv_ref[first, s, jnp.where(is_key, 0, 1), h] = jnp.where(is_key, turned, plain).astype(jnp.bfloat16)
+        return carry
+
+    lax.fori_loop(0, 2 * kv_heads // wide, project_kv, 0)
 
     pair_kv = []
     local = []
@@ -188,11 +181,6 @@
         local.append(pltpu.make_async_copy(kv_ref.at[core, s], kvbuf.at[s, 0, own_sub[s]], loc_sem.at[s]))
     for copy in pair_kv + local:
         copy.start()
-    pair_x = pltpu.make_async_remote_copy(
-        src_ref=x_hbm, dst_ref=x_ref.at[1], send_sem=pair_send.at[2], recv_sem=pair_recv.at[2],
-        device_id=partner, device_id_type=pl.DeviceIdType.MESH)
-    pair_x.start()
-    load_x.start()
     pair_turn = []
     for t, table in enumerate((cos_in, sin_in)):
         local.append(pltpu.make_async_copy(table, turns.at[0, t], loc_sem.at[2 + t]))
@@ -201,10 +189,6 @@
             src_ref=table, dst_ref=turns.at[1, t], send_sem=pair_send.at[6 + t], recv_sem=pair_recv.at[6 + t],
             device_id=partner, device_id_type=pl.DeviceIdType.MESH))
         pair_turn[-1].start()
-
-    acc[...] = jnp.zeros_like(acc)
-    l_ref[...] = jnp.zeros_like(l_ref)
-    m_ref[...] = jnp.full_like(m_ref, NEG)
 
     def held(side, slot):
         twin = plan.twin(pairs[side], slot)
@@ -296,27 +280,7 @@
     echo(0)
 
     mix[...] = spread(n_heads, MIX)
-
-    def sort(block, carry):
-        fetch(block).wait()
-
-        @pl.when(block + 1 < n_blocks)
-        def _():
-            fetch(block + 1).start()
-
-        raw = wraw.at[lax.rem(block, 2)]
-        base = pl.multiple_of(block * depth, depth)
-
-        def arrange(i, c):
-            by_head(mix[...], raw, pl.multiple_of(i * (2 * MIX), 2 * MIX), wsort, n_heads, base)
-            return c
-
-        lax.fori_loop(0, depth * n_heads // (2 * MIX), arrange, 0, unroll=8)
-        return carry
-
-    lax.fori_loop(0, n_blocks, sort, 0)
-    load_x.wait()
-    wide = 2
+    sort(2, n_q, n_heads, lambda: None)
     per_rows = n_heads // wide
 
     def project(i, carry):
@@ -457,8 +421,8 @@
                 def _():
                     prepare()
 
-        doubled = plan.twin(jnp.where(side == 0, pairs[0], pairs[1]), slot) >= 0
-        due = (kind == 0) | ((kind == 1) & jnp.logical_not(doubled)) | ((kind == 2) & doubled)
+        late = plan.twin(jnp.where(side == 0, pairs[0], pairs[1]), slot) > near
+        due = (kind == 0) | ((kind == 1) & jnp.logical_not(late)) | ((kind == 2) & late)
 
         @pl.when(due & (slot < plan.span))
         def _():
@@ -491,10 +455,12 @@
             copy.wait_send()
 
 
-def attend(plan, hidden, w_q, cos, sin, kv_all):
+def attend(plan, hidden, w_q, w_k, w_v, cos, sin):
     model_dim, heads, head_dim = w_q.shape
-    _, _, _, heads_j, chunk, _ = kv_all.shape
-    group = heads // (2 * heads_j)
+    kv_heads = w_k.shape[1]
+    heads_j = kv_heads // 2
+    chunk = hidden.shape[0] // 2
+    group = heads // kv_heads
     bf16, f32 = jnp.bfloat16, jnp.float32
     slots = plan.span + 1
     half_heads = heads // 2
@@ -502,11 +468,12 @@
     vmem = pl.BlockSpec(memory_space=pltpu.VMEM)
     anywhere = pl.BlockSpec(memory_space=pl.ANY)
     return pl.pallas_call(
-        functools.partial(attention_kernel, plan),
+        functools.partial(attention_kernel, plan, kv_heads),
         out_shape=jax.ShapeDtypeStruct((2, chunk, heads * head_dim), bf16),
-        in_specs=[anywhere, anywhere, vmem, vmem, vmem],
+        in_specs=[anywhere, anywhere, anywhere, anywhere, vmem, vmem],
         out_specs=vmem,
         scratch_shapes=[
+            pltpu.VMEM((2, 2, 2, heads_j, chunk, head_dim), bf16),
             pltpu.VMEM((2, 2, heads_j, group, chunk, head_dim), bf16),
             pltpu.VMEM((2, slots, 2, 2, heads_j, chunk, head_dim), bf16),
             pltpu.VMEM((2, 2, heads_j, group, chunk, head_dim), f32),
@@ -529,7 +496,7 @@
         ],
         compiler_params=pltpu.CompilerParams(collective_id=0, has_side_effects=True, vmem_limit_bytes=62 * 1024 * 1024),
         name='attend',
-    )(hidden, w_q.reshape(model_dim, 2, half_heads, head_dim), cos, sin, kv_all)
+    )(hidden, w_k.reshape(-1, half_heads, head_dim), w_v.reshape(-1, half_heads, head_dim), w_q.reshape(model_dim, 2, half_heads, head_dim), cos, sin)
 
 
 def solution(mesh):
@@ -544,8 +511,7 @@
         chunk_ids = jnp.stack([my_index, 2 * cp_size - 1 - my_index])
         positions = (chunk_ids[:, None] * chunk_len + jnp.arange(chunk_len)[None, :]).reshape(2 * chunk_len)
         cos, sin = rotary_tables(positions, head_dim)
-        kv_all = project_kv(hidden, w_k, w_v, cos, sin)
-        attended = attend(plan, hidden, w_q, cos, sin, kv_all)
+        attended = attend(plan, hidden, w_q, w_k, w_v, cos, sin)
         out_rows = jnp.dot(attended.reshape(2 * chunk_len, heads * head_dim), w_o.reshape(heads * head_dim, model_dim), preferred_element_type=jnp.float32)
         return out_rows.astype(jnp.bfloat16)
 

time: 128 us -> 123 us (0.961)
  the two profiles are of different devices: /device:TPU:125 before, /device:TPU:123 now
where the time goes in v5:
time: 123 us
  Pallas kernels  106 us (86%)
  matrix products  14.3 us (12%)
  other arithmetic  2.18 us (2%)
    pallas_call x1, Pallas kernels, attend(): pl.pallas_call(functools.partial(attention_kernel, plan, kv_heads), out_s...  106 us
    dot_general x1, matrix products, device_step(): jnp.dot(attended.reshape(2 * chunk_len, heads * head_dim), w_o.reshape(he...  14.3 us

profile of v5, /device:TPU:123, one launch (start us, length us, event | category | flops | bytes accessed | tf_op | source)
XLA Modules:
  0.0 122.9 jit_solution(10084155798550744912)
XLA Ops:
  0.0 0.1 add_multiply_fusion
  0.1 0.1 convert_bitcast_fusion
  0.2 1.0 fusion
  1.2 1.0 pad_maximum_fusion
  2.2 106.4 %attend.1 = bf16[2,256,2048]{2,1,0:T(8,128)(2,1)} custom-call(bf16[512,4096]{1,0:T(8,128)(2,1)} %x_hbm.1, bf16[2048,8,128]{2,1,0:T(8,128)(2,1)} %bitcast.13, bf16[2048,8,128]{2,1,0:T(8,128)(2,1)} %bitcast.14, bf16[4096,2,8,128]{3,2,1,0:T(8,128)(2,1)} %bitcast.12, f32[512,128]{1,0:T(8,128)} %get-tuple-element.8.cos_in, f32[512,128]{1,0:T(8,128)} %get-tuple-element.9.sin_in), custom_call_target="tpu_custom_call" | custom-call | tf_op jit(solution)/shard_map/attend/pallas_call | solution.py:470
  108.6 14.3 %convolution_convert_fusion = bf16[512,4096]{1,0:T(8,128)(2,1)} fusion(bf16[512,2048]{1,0:T(8,128)(2,1)} %bitcast.15, bf16[2048,4096]{1,0:T(8,128)(2,1)} %bitcast.17), kind=kOutput, calls=%fused_computation | convolution fusion | flops 8592031744 | bytes 23068672 | tf_op jit(solution)/shard_map/dot_general | solution.py:515
  (2 shorter events, 0.0 us)

commit v6 on v5

--- a/solution.py
+++ b/solution.py
@@ -17,9 +17,7 @@
     half_dim = head_dim // 2
     inv_freq = 1.0 / (ROPE_BASE ** (jnp.arange(half_dim, dtype=jnp.float32) * (2.0 / head_dim)))
     angles = positions.astype(jnp.float32)[:, None] * inv_freq
-    cos_part = jnp.cos(angles)
-    sin_part = jnp.sin(angles)
-    return jnp.concatenate([cos_part, cos_part], axis=-1), jnp.concatenate([-sin_part, sin_part], axis=-1)
+    return jnp.cos(angles), jnp.sin(angles)
 
 
 def spread(n_heads, size):
@@ -115,6 +113,8 @@
     fetch(0, 0).start()
     load_x.start()
 
+    turns[0, 0] = jnp.concatenate([cos_in[...], cos_in[...]], axis=1)
+    turns[0, 1] = jnp.concatenate([-sin_in[...], sin_in[...]], axis=1)
     acc[...] = jnp.zeros_like(acc)
     l_ref[...] = jnp.zeros_like(l_ref)
     m_ref[...] = jnp.full_like(m_ref, NEG)
@@ -166,7 +166,7 @@
             rows = slice(s * chunk, (s + 1) * chunk)
             for h in range(wide):
                 plain = part[rows, h * head_dim:(h + 1) * head_dim].astype(jnp.bfloat16).astype(jnp.float32)
-                turned = plain * cos_in[rows] + pltpu.roll(plain, head_dim // 2, 1) * sin_in[rows]
+                turned = plain * turns[0, 0, rows] + pltpu.roll(plain, head_dim // 2, 1) * turns[0, 1, rows]
                 kv_ref[first, s, jnp.where(is_key, 0, 1), h] = jnp.where(is_key, turned, plain).astype(jnp.bfloat16)
         return carry
 
@@ -182,11 +182,9 @@
     for copy in pair_kv + local:
         copy.start()
     pair_turn = []
-    for t, table in enumerate((cos_in, sin_in)):
-        local.append(pltpu.make_async_copy(table, turns.at[0, t], loc_sem.at[2 + t]))
-        local[-1].start()
+    for t in range(2):
         pair_turn.append(pltpu.make_async_remote_copy(
-            src_ref=table, dst_ref=turns.at[1, t], send_sem=pair_send.at[6 + t], recv_sem=pair_recv.at[6 + t],
+            src_ref=turns.at[0, t], dst_ref=turns.at[1, t], send_sem=pair_send.at[6 + t], recv_sem=pair_recv.at[6 + t],
             device_id=partner, device_id_type=pl.DeviceIdType.MESH))
         pair_turn[-1].start()
 
@@ -391,21 +389,26 @@
         return run
 
     def far_events():
-        for s in range(2):
-            event(s, far)
-        for s in range(2):
-            event(s, near, lambda s=s: col_of(s) == 0)
+        arrive(0, plan.span)
+        event(1, far)
+        event(0, near, lambda: col_of(0) == 0)
+        event(0, far)
+
+    def last_events():
+        arrive(1, plan.span)
+        event(0, 2)
+        arrive(0, 7)
 
     def nothing():
         return None
 
     order = [
-        (0, row, 0, nothing), (1, row, 1, nothing),
-        (0, near, 0, far_events), (1, near, 0, nothing), (0, far, 0, nothing), (1, far, 1, nothing),
-        (1, 2, 0, lambda: event(1, 2)), (0, 8, 0, come((0, 8))), (0, 2, 0, lambda: event(0, 2)),
-        (1, row, 2, nothing), (1, far, 2, nothing),
-        (0, 5, 0, come((0, 5))), (1, 5, 0, come((1, 5))), (0, 7, 0, come((0, 7))), (1, 8, 0, come((1, 8))),
-        (0, 6, 0, come((0, 6))), (1, 7, 0, lambda: (low_done(), arrive(1, 7))), (1, 6, 0, come((1, 6))),
+        (0, row, 0, nothing), (1, row, 1, nothing), (1, near, 0, lambda: event(1, near, lambda: col_of(1) == 0)),
+        (0, 8, 0, far_events), (1, far, 1, nothing), (0, far, 0, nothing), (0, near, 0, nothing),
+        (0, 5, 0, come((0, 5))), (1, 5, 1, come((1, 5))), (1, 2, 0, lambda: event(1, 2)),
+        (1, 8, 0, last_events), (0, 7, 0, nothing), (0, 2, 0, nothing),
+        (1, row, 2, nothing), (1, far, 2, nothing), (1, 5, 2, nothing),
+        (0, 6, 0, come((0, 6), (1, 7))), (1, 7, 0, low_done), (1, 6, 0, come((1, 6))),
     ]
 
     def visit(i, carry):
@@ -486,7 +489,7 @@
             pltpu.VMEM((MIX, MIX), bf16),
             pltpu.VMEM((2, depth, half_heads, head_dim), bf16),
             pltpu.VMEM((model_dim, half_heads * head_dim), bf16),
-            pltpu.SemaphoreType.DMA((4,)),
+            pltpu.SemaphoreType.DMA((2,)),
             pltpu.SemaphoreType.DMA,
             pltpu.SemaphoreType.DMA((2,)),
             pltpu.SemaphoreType.DMA((8,)),

time: 123 us -> 121 us (0.984)
    pallas_call x1, Pallas kernels: 106 us -> 105 us  [attend(): pl.pallas_call(functools.partial(attention_kernel, plan, kv_heads), out_s...]
    sin x0 -> x1, other arithmetic: none -> 1.79 us  [rotary_tables(): return (jnp.cos(angles), jnp.sin(angles))]
where the time goes in v6:
time: 121 us
  Pallas kernels  105 us (87%)
  matrix products  14.3 us (12%)
  other arithmetic  1.95 us (2%)
    pallas_call x1, Pallas kernels, attend(): pl.pallas_call(functools.partial(attention_kernel, plan, kv_heads), out_s...  105 us
    dot_general x1, matrix products, device_step(): jnp.dot(attended.reshape(2 * chunk_len, heads * head_dim), w_o.reshape(he...  14.3 us

profile of v6, /device:TPU:123, one launch (start us, length us, event | category | flops | bytes accessed | tf_op | source)
XLA Modules:
  0.0 120.8 jit_solution(3409485184733488257)
XLA Ops:
  0.0 0.1 add_multiply_fusion
  0.1 0.1 convert_bitcast_fusion
  0.2 1.8 %multiply_sine_fusion = (f32[512,64]{1,0:T(8,128)}, f32[512,64]{1,0:T(8,128)}) fusion(f32[64]{0:T(128)S(1)} %negate_power_fusion, f32[512]{0:T(512)S(1)} %bitcast.16), kind=kLoop, calls=%fused_computation.1 | loop fusion | flops 32768 | bytes 264448 | tf_op jit(solution)/shard_map/sin | solution.py:20
  2.0 104.5 %attend.1 = bf16[2,256,2048]{2,1,0:T(8,128)(2,1)} custom-call(bf16[512,4096]{1,0:T(8,128)(2,1)} %x_hbm.1, bf16[2048,8,128]{2,1,0:T(8,128)(2,1)} %bitcast.13, bf16[2048,8,128]{2,1,0:T(8,128)(2,1)} %bitcast.14, bf16[4096,2,8,128]{3,2,1,0:T(8,128)(2,1)} %bitcast.12, f32[512,64]{1,0:T(8,128)} %get-tuple-element.6.cos_in, f32[512,64]{1,0:T(8,128)} %get-tuple-element.5.sin_in), custom_call_target="tpu_custom_call" | custom-call | tf_op jit(solution)/shard_map/attend/pallas_call | solution.py:473
  106.5 14.3 %convolution_convert_fusion = bf16[512,4096]{1,0:T(8,128)(2,1)} fusion(bf16[512,2048]{1,0:T(8,128)(2,1)} %bitcast.15, bf16[2048,4096]{1,0:T(8,128)(2,1)} %bitcast.17), kind=kOutput, calls=%fused_computation | convolution fusion | flops 8592031744 | bytes 23068672 | tf_op jit(solution)/shard_map/dot_general | solution.py:518
  (2 shorter events, 0.0 us)

commit v7 on v6

--- a/solution.py
+++ b/solution.py
@@ -142,7 +142,7 @@
                 by_head(mix[...], raw, pl.multiple_of(i * (2 * MIX), 2 * MIX), wsort, heads, base, width if part == 1 else 0)
                 return c
 
-            lax.fori_loop(0, depth * raw.shape[1] // (2 * MIX), arrange, 0, unroll=8)
+            lax.fori_loop(0, depth * raw.shape[1] // (2 * MIX), arrange, 0, unroll=16)
             return carry
 
         lax.fori_loop(0, blocks, step, 0)
@@ -312,30 +312,31 @@
     def block(side, slot_side, slot, j, subs, masked, edge):
         k = kvbuf[slot_side, slot, :, 0, j].reshape(2 * chunk, head_dim)
         v = kvbuf[slot_side, slot, :, 1, j].reshape(2 * chunk, head_dim)
-        tiles = [(a, g) for a in subs for g in range(group)]
+        tiles = list(subs)
+        tall = group * chunk
 
         def score(t):
-            a, g = tiles[t]
-            return lax.dot_general(qbuf[side, a, j, g], k, (((1,), (1,)), ((), ())), preferred_element_type=jnp.float32)
+            return lax.dot_general(qbuf[side, tiles[t], j].reshape(tall, head_dim), k, (((1,), (1,)), ((), ())), preferred_element_type=jnp.float32)
 
         def update(t, s):
-            a, g = tiles[t]
+            a = tiles[t]
             if masked:
-                rows = lax.broadcasted_iota(jnp.int32, (chunk, 2 * chunk), 0) + a * chunk
-                cols = lax.broadcasted_iota(jnp.int32, (chunk, 2 * chunk), 1)
+                rows = lax.broadcasted_iota(jnp.int32, (tall, 2 * chunk), 0) % chunk + a * chunk
+                cols = lax.broadcasted_iota(jnp.int32, (tall, 2 * chunk), 1)
                 s = jnp.where((cols > rows) if edge else (cols <= rows), s, NEG)
-            m_old = m_ref[side, a, j, g]
+            m_old = m_ref[side, a, j].reshape(tall, head_dim)
             m_new = jnp.maximum(m_old, jnp.max(s, axis=1, keepdims=True))
             alpha = jnp.exp(m_old - m_new)
             e = jnp.exp(s - jnp.concatenate([m_new] * (2 * chunk // m_new.shape[1]), axis=1))
             part = e[:, :head_dim]
             for b in range(1, 2 * chunk // head_dim):
                 part = part + e[:, b * head_dim:(b + 1) * head_dim]
-            m_ref[side, a, j, g] = m_new
-            l_ref[side, a, j, g] = l_ref[side, a, j, g] * alpha + part
-            acc[side, a, j, g] = acc[side, a, j, g] * alpha + jnp.dot(e.astype(jnp.bfloat16), v, preferred_element_type=jnp.float32)
-
-        ahead = 2
+            m_ref[side, a, j] = m_new.reshape(group, chunk, head_dim)
+            l_ref[side, a, j] = (l_ref[side, a, j].reshape(tall, head_dim) * alpha + part).reshape(group, chunk, head_dim)
+            total = acc[side, a, j].reshape(tall, head_dim) * alpha + jnp.dot(e.astype(jnp.bfloat16), v, preferred_element_type=jnp.float32)
+            acc[side, a, j] = total.reshape(group, chunk, head_dim)
+
+        ahead = 1
         scores = [score(t) for t in range(ahead)]
         for t in range(len(tiles)):
             if t + ahead < len(tiles):

time: 121 us -> 120 us (level)
  Pallas kernels: 105 us -> 103 us
    pallas_call x1, Pallas kernels: 105 us -> 103 us  [attend(): pl.pallas_call(functools.partial(attention_kernel, plan, kv_heads), out_s...]
where the time goes in v7:
time: 120 us; the launch traced here: 119 us
  Pallas kernels  103 us (86%)
  matrix products  14.3 us (12%)
  other arithmetic  1.95 us (2%)
    pallas_call x1, Pallas kernels, attend(): pl.pallas_call(functools.partial(attention_kernel, plan, kv_heads), out_s...  103 us
    dot_general x1, matrix products, device_step(): jnp.dot(attended.reshape(2 * chunk_len, heads * head_dim), w_o.reshape(he...  14.3 us

profile of v7, /device:TPU:123, one launch (start us, length us, event | category | flops | bytes accessed | tf_op | source)
XLA Modules:
  0.0 119.3 jit_solution(16098376828782164348)
XLA Ops:
  0.0 0.1 add_multiply_fusion
  0.1 0.1 convert_bitcast_fusion
  0.2 1.8 %multiply_sine_fusion = (f32[512,64]{1,0:T(8,128)}, f32[512,64]{1,0:T(8,128)}) fusion(f32[64]{0:T(128)S(1)} %negate_power_fusion, f32[512]{0:T(512)S(1)} %bitcast.16), kind=kLoop, calls=%fused_computation.1 | loop fusion | flops 32768 | bytes 264448 | tf_op jit(solution)/shard_map/sin | solution.py:20
  2.0 103.0 %attend.1 = bf16[2,256,2048]{2,1,0:T(8,128)(2,1)} custom-call(bf16[512,4096]{1,0:T(8,128)(2,1)} %x_hbm.1, bf16[2048,8,128]{2,1,0:T(8,128)(2,1)} %bitcast.13, bf16[2048,8,128]{2,1,0:T(8,128)(2,1)} %bitcast.14, bf16[4096,2,8,128]{3,2,1,0:T(8,128)(2,1)} %bitcast.12, f32[512,64]{1,0:T(8,128)} %get-tuple-element.6.cos_in, f32[512,64]{1,0:T(8,128)} %get-tuple-element.5.sin_in), custom_call_target="tpu_custom_call" | custom-call | tf_op jit(solution)/shard_map/attend/pallas_call | solution.py:474
  105.0 14.3 %convolution_convert_fusion = bf16[512,4096]{1,0:T(8,128)(2,1)} fusion(bf16[512,2048]{1,0:T(8,128)(2,1)} %bitcast.15, bf16[2048,4096]{1,0:T(8,128)(2,1)} %bitcast.17), kind=kOutput, calls=%fused_computation | convolution fusion | flops 8592031744 | bytes 23068672 | tf_op jit(solution)/shard_map/dot_general | solution.py:519
  (2 shorter events, 0.0 us)
